TPU v7x, 64 devices: a 2x2x8 block of a 4x4x8 slice. The times are simulated.
64 devices in a mesh: dp: 4 (over x, y), sp: 16 (over z, core).
Axes of the slice: x: 2, y: 2, z: 8, core: 2. Of those that a mesh axis runs over, the one named last changes fastest.
The devices are a block of a 4x4x8 slice.
Arguments:
- hidden: bfloat16 [128, 512, 2048], P('dp', 'sp'), parts along dimension 0
- seq_lens: int32 [128], P('dp'), parts along dimension 0
- ln1_gain: float32 [2048], replicated
- ln1_bias: float32 [2048], replicated
- ln2_gain: float32 [2048], replicated
- ln2_bias: float32 [2048], replicated
- w_qkv: bfloat16 [2048, 6144], replicated
- b_qkv: float32 [16, 3, 128], replicated
- w_out: bfloat16 [2048, 2048], replicated
- b_out: float32 [2048], replicated
- w_up: bfloat16 [2048, 8192], replicated
- b_up: float32 [8192], replicated
- w_down: bfloat16 [8192, 2048], replicated
- b_down: float32 [2048], replicated
Outputs:
- output 1: bfloat16 [128, 512, 2048], P('dp', 'sp'), parts along dimension 0
- output 2: bfloat16 [128, 16, 512, 128], P('dp', 'sp'), parts along dimension 0
- output 3: bfloat16 [128, 16, 512, 128], P('dp', 'sp'), parts along dimension 0
There are 4 independent parts. A program takes and returns all parts, laid end to end along the dimension named above; an argument that names none is the same for every part.
All inputs are finite; a program needn't handle non-finite values.
Results may differ from a plain program's by a relative error of at most 0.00254755.
Values are sent between devices in bfloat16 or wider.
A program may use at most 768 MiB of HBM per device.

v0:
```python
import jax
import jax.numpy as jnp
from jax import lax
from jax.sharding import PartitionSpec as P

LN_EPS = 1e-5
ROT_BASE = 10000.0


def layer_norm(rows, gain, shift):
    rows32 = rows.astype(jnp.float32)
    centered = rows32 - jnp.mean(rows32, axis=-1, keepdims=True)
    variance = jnp.mean(centered * centered, axis=-1, keepdims=True)
    return (centered * lax.rsqrt(variance + LN_EPS) * gain + shift).astype(jnp.bfloat16)


def rotary_tables(positions, head_dim):
    rot_dim = head_dim // 4
    half_rot = rot_dim // 2
    inv_freq = ROT_BASE ** (-2.0 * jnp.arange(half_rot, dtype=jnp.float32) / rot_dim)
    angles = positions.astype(jnp.float32)[:, None] * inv_freq[None, :]
    return jnp.cos(angles), jnp.sin(angles)


def rotary(vecs, cosines, sines):
    half_rot = cosines.shape[-1]
    first = vecs[..., :half_rot]
    second = vecs[..., half_rot:2 * half_rot]
    return jnp.concatenate([first * cosines - second * sines, second * cosines + first * sines, vecs[..., 2 * half_rot:]], axis=-1)


def solution(mesh):
    n_shards = mesh.shape['sp']
    row_spec = P('dp', 'sp', None)
    cache_spec = P('dp', 'sp', None, None)
    vec_spec = P(None)
    mat_spec = P(None, None)

    def local_layer(hidden, seq_lens, ln1_gain, ln1_bias, ln2_gain, ln2_bias, w_qkv, b_qkv, w_out, b_out, w_up, b_up, w_down, b_down):
        n_prompts, rows_dev, d_model = hidden.shape
        n_heads = b_qkv.shape[0]
        head_dim = b_qkv.shape[2]
        seq_len = rows_dev * n_shards
        shard = lax.axis_index('sp')
        attn_in = layer_norm(hidden, ln1_gain, ln1_bias)
        mlp_in = layer_norm(hidden, ln2_gain, ln2_bias)
        proj_qkv = jnp.einsum('btd,de->bte', attn_in, w_qkv, preferred_element_type=jnp.float32)
        proj_qkv = proj_qkv.reshape(n_prompts, rows_dev, n_heads, 3, head_dim) + b_qkv
        positions = shard * rows_dev + jnp.arange(rows_dev)
        cosines, sines = rotary_tables(positions, head_dim)
        rotated = rotary(proj_qkv[:, :, :, :2], cosines[:, None, None, :], sines[:, None, None, :])
        packed = jnp.concatenate([rotated, proj_qkv[:, :, :, 2:]], axis=3).astype(jnp.bfloat16)
        by_heads = lax.all_to_all(packed, 'sp', 2, 1, tiled=True)
        q_heads = jnp.transpose(by_heads[:, :, :, 0], (0, 2, 1, 3))
        k_cache = jnp.transpose(by_heads[:, :, :, 1], (0, 2, 1, 3))
        v_cache = jnp.transpose(by_heads[:, :, :, 2], (0, 2, 1, 3))
        key_pos = jnp.arange(seq_len)
        score_scale = head_dim ** -0.5

        def one_block(start):
            q_blk = lax.dynamic_slice_in_dim(q_heads, start, rows_dev, axis=2)
            scores = jnp.einsum('bhqd,bhkd->bhqk', q_blk, k_cache, preferred_element_type=jnp.float32) * score_scale
            q_pos = start + jnp.arange(rows_dev)
            allowed = (key_pos[None, None, :] <= q_pos[None, :, None]) & (key_pos[None, None, :] < seq_lens[:, None, None])
            scores = jnp.where(allowed[:, None], scores, -jnp.inf)
            weights = jnp.exp(scores - jnp.max(scores, axis=-1, keepdims=True))
            total = jnp.sum(weights, axis=-1)
            context = jnp.einsum('bhqk,bhkd->bqhd', weights.astype(jnp.bfloat16), v_cache, preferred_element_type=jnp.float32)
            context = context / jnp.transpose(total, (0, 2, 1))[:, :, :, None]
            return context.astype(jnp.bfloat16)

        ctx_blocks = lax.map(one_block, jnp.arange(n_shards) * rows_dev)
        ctx_rows = lax.all_to_all(ctx_blocks, 'sp', 0, 3, tiled=True)
        ctx_flat = ctx_rows.reshape(n_prompts * rows_dev, d_model)
        attn_out = jnp.dot(ctx_flat, w_out, preferred_element_type=jnp.float32) + b_out
        pre_act = jnp.dot(mlp_in.reshape(n_prompts * rows_dev, d_model), w_up, preferred_element_type=jnp.float32) + b_up
        hidden_act = jax.nn.gelu(pre_act, approximate=False).astype(jnp.bfloat16)
        mlp_out = jnp.dot(hidden_act, w_down, preferred_element_type=jnp.float32) + b_down
        summed = hidden.reshape(n_prompts * rows_dev, d_model).astype(jnp.float32) + attn_out + mlp_out
        return summed.astype(jnp.bfloat16).reshape(n_prompts, rows_dev, d_model), k_cache, v_cache

    return jax.shard_map(local_layer, mesh=mesh,
                         in_specs=(row_spec, P('dp'), vec_spec, vec_spec, vec_spec, vec_spec, mat_spec, P(None, None, None), mat_spec, vec_spec, mat_spec, vec_spec, mat_spec, vec_spec),
                         out_specs=(row_spec, cache_spec, cache_spec), check_vma=False)
```

profile of v0, /device:TPU:21, one launch (start us, length us, event | category | flops | bytes accessed | tf_op | source)
XLA Modules:
  0.0 906.1 jit_solution(13467868946601738186)
XLA Ops:
  7.4 32.9 %fusion.40 = f32[32,32,6144]{2,1,0:T(8,128)} fusion(bf16[2048,6144]{1,0:T(8,128)(2,1)} %param.22, bf16[32,32,2048]{2,1,0:T(8,128)(2,1)} %param.16, f32[2048]{0:T(1024)} %param.19, f32[2048]{0:T(1024)} %param.18, f32[32,32]{1,0:T(8,128)S(1)} %add_rsqrt_fusion, f32[32,32]{1,0:T(8,128)S(1)} %broadcast_multiply_fusion), kind=kOutput, calls=%fused_computation.40 | convolution fusion | flops 25782386688 | bytes 54550528 | tf_op jit(solution)/shard_map/btd,de->bte/dot_general | solution.py:47
  40.3 40.9 %reshape.197 = f32[32,32,16,3,128]{4,3,2,1,0:T(4,128)} reshape(f32[32,32,6144]{2,1,0:T(8,128)} %fusion.40) | data formatting | bytes 50331648 | tf_op jit(solution)/shard_map/reshape | solution.py:48
  81.3 29.2 %fusion.87 = (bf16[32,32,16,3,128]{4,3,2,1,0:T(4,128)(2,1)}, f32[32,32,16,3,128]{4,3,2,1,0:T(4,128)}) fusion(f32[32,32,16,3,128]{4,3,2,1,0:T(4,128)} %reshape.197, f32[16,3,128]{2,1,0:T(4,128)S(1)} %copy.30), kind=kLoop, calls=%fused_computation.104 | loop fusion | flops 12582912 | bytes 62939136 | tf_op jit(solution)/shard_map/convert.7
  110.5 12.7 %slice.36 = bf16[32,32,16,2,96]{4,3,2,1,0:T(2,128)(2,1)} slice(bf16[32,32,16,3,128]{4,3,2,1,0:T(4,128)(2,1)} %get-tuple-element.119), slice={[0:32], [0:32], [0:16], [0:2], [32:128]} | slice | bytes 12582912 | tf_op jit(solution)/shard_map/slice | solution.py:29
  124.2 10.5 %slice.37 = bf16[32,32,16,1,128]{4,3,2,1,0:T(2,128)(2,1)} slice(bf16[32,32,16,3,128]{4,3,2,1,0:T(4,128)(2,1)S(1)} %copy-done), slice={[0:32], [0:32], [0:16], [2:3], [0:128]} | slice | bytes 8388608 | tf_op jit(solution)/shard_map/slice | solution.py:52
  134.8 28.2 %subtract_convert_fusion = (bf16[32,32,16,2,16]{4,3,2,1,0:T(2,128)(2,1)}, bf16[32,32,16,2,16]{4,3,2,1,0:T(2,128)(2,1)}) fusion(f32[32,32,16,3,128]{4,3,2,1,0:T(4,128)} %get-tuple-element.120, f32[32,16]{1,0:T(8,128)S(1)} %get-tuple-element.133, f32[32,16]{1,0:T(8,128)S(1)} %get-tuple-element.132), kind=kLoop, calls=%fused_computation.44 | loop fusion | flops 4194304 | bytes 6295552 | tf_op jit(solution)/shard_map/convert.4
  163.0 50.5 %pad_maximum_fusion = bf16[32,32,16,3,128]{4,3,2,1,0:T(4,128)(2,1)} fusion(bf16[32,32,16,1,128]{4,3,2,1,0:T(2,128)(2,1)} %slice.37, bf16[32,32,16,2,96]{4,3,2,1,0:T(2,128)(2,1)} %slice.36, bf16[32,32,16,2,16]{4,3,2,1,0:T(2,128)(2,1)} %get-tuple-element.126, bf16[32,32,16,2,16]{4,3,2,1,0:T(2,128)(2,1)} %get-tuple-element.125), kind=kLoop, calls=%fused_computation.42 | loop fusion | flops 50331648 | bytes 25165824 | tf_op jit(solution)/shard_map/concatenate | solution.py:52
  213.5 18.0 %copy.31 = bf16[32,32,16,3,128]{4,1,3,0,2:T(8,128)(2,1)} copy(bf16[32,32,16,3,128]{4,3,2,1,0:T(4,128)(2,1)} %pad_maximum_fusion) | data formatting | bytes 25165824 | tf_op jit(solution)/shard_map/concatenate | solution.py:52
  231.5 10.8 %all-to-all-start = ((bf16[32,32,16,3,128]{4,1,3,0,2:T(8,128)(2,1)}), bf16[32,32,16,3,128]{4,1,3,0,2:T(8,128)(2,1)}, u32[]{:S(2)}, u32[]{:S(2)}) async-start(bf16[32,32,16,3,128]{4,1,3,0,2:T(8,128)(2,1)} %copy.31), calls=%async_computation | async-start | bytes 25165824 | tf_op jit(solution)/shard_map/all_to_all | solution.py:53
  242.4 4.6 add_convert_fusion.1
  247.0 280.0 %all-to-all-done = bf16[32,32,16,3,128]{4,1,3,0,2:T(8,128)(2,1)} async-done(((bf16[32,32,16,3,128]{4,1,3,0,2:T(8,128)(2,1)}), bf16[32,32,16,3,128]{4,1,3,0,2:T(8,128)(2,1)}, u32[]{:S(2)}, u32[]{:S(2)}) %all-to-all-start) | async-done | bytes 12582944 | tf_op jit(solution)/shard_map/all_to_all | solution.py:53
  526.9 7.5 copy.32
  534.5 8.1 slice_bitcast_fusion.1
  542.6 181.4 %while.12 = (s32[]{:T(128)}, bf16[16,32,32,1,128]{4,2,1,3,0:T(8,128)(2,1)}, s32[16]{0:T(128)S(1)}, s32[32]{0:T(128)S(1)}, bf16[32,1,512,128]{3,2,0,1:T(8,128)(2,...) while((s32[]{:T(128)}, ...), condition=%wide.region_5.6_spmd.clone.clone, body=%wide.region_2.5_spmd.clone.clone.sunk | while | flops 272922656 | bytes 15291419 | solution.py:72
  545.5 3.9 fusion.111
  550.1 3.8 fusion.113
  556.8 3.9 fusion.111
  561.4 3.8 fusion.113
  568.1 3.9 fusion.111
  572.8 3.8 fusion.113
  579.5 3.9 fusion.111
  584.1 3.8 fusion.113
  590.8 3.9 fusion.111
  595.4 3.8 fusion.113
  602.1 3.9 fusion.111
  613.5 3.9 fusion.111
  618.1 3.8 fusion.113
  624.8 3.9 fusion.111
  629.5 3.8 fusion.113
  636.1 3.9 fusion.111
  640.8 3.8 fusion.113
  647.5 3.9 fusion.111
  652.1 3.8 fusion.113
  658.8 3.9 fusion.111
  663.5 3.8 fusion.113
  670.1 3.9 fusion.111
  681.5 3.9 fusion.111
  686.1 3.8 fusion.113
  692.8 3.9 fusion.111
  704.1 3.9 fusion.111
  708.8 3.8 fusion.113
  715.5 3.9 fusion.111
  720.1 3.8 fusion.113
  723.9 6.7 all-to-all-start.1
  730.6 109.2 %fusion.102 = bf16[1024,8192]{1,0:T(8,128)(2,1)} fusion(f32[8192]{0:T(1024)S(1)} %copy-done.7, bf16[1024,2048]{1,0:T(8,128)(2,1)} %bitcast.107, bf16[2048,8192]{1,0:T(8,128)(2,1)} %param.26), kind=kOutput, calls=%fused_computation.24.clone.clone.clone.clone.1 | convolution fusion | flops 34913386496 | bytes 54558720 | tf_op jit(solution)/shard_map/dot_general | solution.py:76
  839.8 7.0 copy.33
  846.9 13.3 %fusion.48 = f32[1024,2048]{1,0:T(8,128)} fusion(bf16[2048,2048]{1,0:T(8,128)(2,1)} %param.24, bf16[128,8,16,128]{3,2,1,0:T(8,128)(2,1)S(1)} %bitcast.108), kind=kOutput, calls=%fused_computation.55 | convolution fusion | flops 8589934592 | bytes 20971520 | tf_op jit(solution)/shard_map/dot_general | solution.py:75
  860.3 45.6 %fusion.47 = bf16[1024,2048]{1,0:T(8,128)(2,1)} fusion(f32[1024,2048]{1,0:T(8,128)} %fusion.48, bf16[32,32,2048]{2,1,0:T(8,128)(2,1)S(1)} %copy-done.1, f32[2048]{0:T(1024)S(1)} %copy-done.8, f32[2048]{0:T(1024)S(1)} %copy-done.9, bf16[8192,2048]{1,0:T(8,128)(2,1)} %param.28, bf16[1024,8192]{1,0:T(8,128)(2,1)} %fusion.102), kind=kOutput, calls=%fused_computation.50 | convolution fusion | flops 34372321280 | bytes 67125248 | tf_op jit(solution)/shard_map/dot_general | solution.py:78
  (98 shorter events, 50.0 us)
Async XLA Ops:
  40.3 40.9 %copy-start.2 = (f32[16,3,128]{2,0,1:T(8,128)S(1)}, f32[16,3,128]{2,0,1:T(8,128)}, u32[]{:S(2)}) copy-start(f32[16,3,128]{2,0,1:T(8,128)} %param.23) | copy-start | bytes 73732
  110.5 13.7 %copy-start = (bf16[32,32,16,3,128]{4,3,2,1,0:T(4,128)(2,1)S(1)}, bf16[32,32,16,3,128]{4,3,2,1,0:T(4,128)(2,1)}, u32[]{:S(2)}) copy-start(bf16[32,32,16,3,128]{4,3,2,1,0:T(4,128)(2,1)} %get-tuple-element.119) | copy-start | bytes 37748740
  110.5 24.2 %copy-start.6 = (f32[16]{0:T(128)S(1)}, f32[16]{0:T(128)}, u32[]{:S(2)}) copy-start(f32[16]{0:T(128)} %multiply_power_fusion) | copy-start | bytes 196
  231.5 10.9 %copy-start.4 = (f32[2048]{0:T(1024)S(1)}, f32[2048]{0:T(1024)}, u32[]{:S(2)}) copy-start(f32[2048]{0:T(1024)} %param.21) | copy-start | bytes 24580
  231.5 10.9 %copy-start.5 = (f32[2048]{0:T(1024)S(1)}, f32[2048]{0:T(1024)}, u32[]{:S(2)}) copy-start(f32[2048]{0:T(1024)} %param.20) | copy-start | bytes 24580
  231.5 295.4 %all-to-all-start = ((bf16[32,32,16,3,128]{4,1,3,0,2:T(8,128)(2,1)}), bf16[32,32,16,3,128]{4,1,3,0,2:T(8,128)(2,1)}, u32[]{:S(2)}, u32[]{:S(2)}) async-start(bf16[32,32,16,3,128]{4,1,3,0,2:T(8,128)(2,1)} %copy.31), calls=%async_computation | async-start | bytes 25165824 | tf_op jit(solution)/shard_map/all_to_all | solution.py:53
  534.5 8.1 copy-start.3
  542.6 188.0 %copy-start.7 = (f32[8192]{0:T(1024)S(1)}, f32[8192]{0:T(1024)}, u32[]{:S(2)}) copy-start(f32[8192]{0:T(1024)} %param.27) | copy-start | bytes 98308
  723.9 115.9 %all-to-all-start.1 = ((bf16[16,32,32,1,128]{4,2,1,3,0:T(8,128)(2,1)}), bf16[16,32,32,1,128]{4,2,1,3,0:T(8,128)(2,1)}, u32[]{:S(2)}, u32[]{:S(2)}) async-start(bf16[16,32,32,1,128]{4,2,1,3,0:T(8,128)(2,1)} %get-tuple-element.48), calls=%async_computation.1 | async-start | bytes 8388608 | tf_op jit(solution)/shard_map/all_to_all | solution.py:73
  846.9 13.4 %copy-start.1 = (bf16[32,32,2048]{2,1,0:T(8,128)(2,1)S(1)}, bf16[32,32,2048]{2,1,0:T(8,128)(2,1)}, u32[]{:S(2)}) copy-start(bf16[32,32,2048]{2,1,0:T(8,128)(2,1)} %param.16) | copy-start | bytes 12582916
  846.9 13.4 %copy-start.8 = (f32[2048]{0:T(1024)S(1)}, f32[2048]{0:T(1024)}, u32[]{:S(2)}) copy-start(f32[2048]{0:T(1024)} %param.29) | copy-start | bytes 24580
  846.9 13.4 %copy-start.9 = (f32[2048]{0:T(1024)S(1)}, f32[2048]{0:T(1024)}, u32[]{:S(2)}) copy-start(f32[2048]{0:T(1024)} %param.25) | copy-start | bytes 24580
where the time goes:
time: 918 us; the launch traced here: 906 us
  matrix products  325 us (35%)
  waiting for transfers between devices  280 us (31%)
  other arithmetic  141 us (15%)
  local copies, waits for them, and re-layouts  115 us (13%)
  loops' own time  26.8 us (3%)
  starting transfers between devices  17.5 us (2%)
    all_to_all x1, waiting for transfers between devices, local_layer(): by_heads = lax.all_to_all(packed, 'sp', 2, 1, tiled=True)  280 us
    dot_general x1, matrix products, local_layer(): jnp.dot(mlp_in.reshape(n_prompts * rows_dev, d_model), w_up, preferred_el...  109 us
    dot_general x16, matrix products, one_block(): jnp.einsum('bhqd,bhkd->bhqk', q_blk, k_cache, preferred_element_type=jnp....  62.9 us
    dot_general x16, matrix products, one_block(): jnp.einsum('bhqk,bhkd->bqhd', weights.astype(jnp.bfloat16), v_cache, pref...  61.1 us
    another operation x2, other arithmetic  57.4 us
    concatenate x1, other arithmetic, local_layer(): jnp.concatenate([rotated, proj_qkv[:, :, :, 2:]], axis=3)  50.5 us
    dot_general x1, matrix products, local_layer(): jnp.dot(hidden_act, w_down, preferred_element_type=jnp.float32) + b_down  45.6 us
    reshape x1, local copies, waits for them, and re-layouts, local_layer(): proj_qkv.reshape(n_prompts, rows_dev, n_heads, 3, head_dim) + b_qkv  40.9 us
  transfers between devices with their start and end apart: 2, of which 1 were waited for; matrix products, arithmetic and copies ran while one was open for 13% of the time, Pallas kernels for 0%

commit v1 on v0

v1 whole, which is shorter than its diff:
```python
import functools

import jax
import jax.numpy as jnp
import numpy as np
from jax import lax
from jax.experimental import pallas as pl
from jax.experimental.pallas import tpu as pltpu
from jax.sharding import PartitionSpec as P

LN_EPS = 1e-5
ROT_BASE = 10000.0
PC = 4
AHEAD = 3
FB = 512
MESH = pl.DeviceIdType.MESH
VMEM_LIMIT = 66_900_000
ANY = pl.BlockSpec(memory_space=pl.ANY)
VM = pl.BlockSpec(memory_space=pltpu.VMEM)
SM = pl.BlockSpec(memory_space=pltpu.SMEM)


def rotary_tables(seq_len, head_dim):
    rot = head_dim // 4
    half = rot // 2
    inv = np.float32(ROT_BASE) ** (np.float32(-2.0) * np.arange(half, dtype=np.float32) / np.float32(rot))
    ang = np.arange(seq_len, dtype=np.float32)[:, None] * inv[None, :].astype(np.float32)
    cos, sin = np.cos(ang), np.sin(ang)
    c = np.ones((seq_len, head_dim), np.float32)
    s = np.zeros((2, seq_len, head_dim), np.float32)
    c[:, :half] = cos
    c[:, half:rot] = cos
    s[0, :, :half] = -sin
    s[1, :, half:rot] = sin
    return c, s[0], s[1]


def entry_barrier(n, me):
    sem = pltpu.get_barrier_semaphore()
    for d in range(1, n):
        pl.semaphore_signal(sem, inc=1, device_id={'sp': lax.rem(me + d, n)}, device_id_type=MESH)
    return lambda: pl.semaphore_wait(sem, n - 1)


def project_kernel(n, hid, g1, s1, g2, s2, wqkv, bqkv, tab_c, tab_l, tab_r, wup, bup, wdn, bsum,
                   q_out, k_out, v_out, acc_out,
                   a_own, a_nb, m_buf, acc, w_sc, wup_b, wdn_b, st,
                   x_sem, w_sem, up_sem, dn_sem, a_send, a_recv, st_sem, self_sem, r_sem, o_sem):
    me = lax.axis_index('sp')
    chip = lax.div(me, 2)
    n_prompts, tok, d_model = hid.shape
    hd = q_out.shape[3]
    wide = 3 * hd
    n_chunks = n_prompts // PC
    rows = PC * tok
    n_far = n // 2 - 3
    n_loc = n_far + 2
    n_w = 2 * n_far + 2
    n_fb = bup.shape[0]
    fb = bup.shape[2]
    outs = (q_out, k_out, v_out)

    await_barrier = entry_barrier(n, me)

    def x_copy(i):
        r = pl.multiple_of(i * rows, rows)
        return pltpu.make_async_copy(hid.at[pl.ds(i * PC, PC)], m_buf.at[pl.ds(i * PC, PC)], x_sem.at[i])

    def w_copy(j):
        head = lax.rem(2 * chip - n_far + j + n, n)
        return pltpu.make_async_copy(wqkv.at[:, pl.ds(pl.multiple_of(head * wide, 128), wide)], w_sc.at[j], w_sem.at[j])

    def up_copy(j, slot):
        return pltpu.make_async_copy(wup.at[:, pl.ds(pl.multiple_of(j * fb, 128), fb)], wup_b.at[slot], up_sem.at[slot])

    def dn_copy(j, slot):
        return pltpu.make_async_copy(wdn.at[pl.ds(pl.multiple_of(j * fb, 128), fb)], wdn_b.at[slot], dn_sem.at[slot])

    @pl.loop(0, n_chunks)
    def _(i):
        x_copy(i).start()

    @pl.loop(0, n_w)
    def _(j):
        w_copy(j).start()

    for j in range(2):
        up_copy(j, j).start()
        dn_copy(j, j).start()

    def a_copy(side, i):
        to = lax.rem(me + (2 if side == 0 else n - 2), n)
        r = pl.ds(pl.multiple_of(i * rows, rows), rows)
        return pltpu.make_async_remote_copy(
            src_ref=a_own.at[r], dst_ref=a_nb.at[side, r], send_sem=a_send.at[side, i], recv_sem=a_recv.at[side, i],
            device_id={'sp': to}, device_id_type=MESH)

    def norm_chunk(i):
        x_copy(i).wait()
        r = pl.ds(pl.multiple_of(i * rows, rows), rows)
        pr = pl.ds(i * PC, PC)
        x = m_buf[pr].reshape(rows, d_model).astype(jnp.float32)
        cen = x - jnp.mean(x, axis=-1, keepdims=True)
        var = jnp.mean(cen * cen, axis=-1, keepdims=True)
        nor = cen * lax.rsqrt(var + LN_EPS)
        a_own[r] = (nor * g1[...] + s1[...]).astype(jnp.bfloat16)
        m_buf[pr] = (nor * g2[...] + s2[...]).astype(jnp.bfloat16).reshape(PC, tok, d_model)
        acc[r] = x + bsum[...]

    norm_chunk(0)
    await_barrier()
    for side in range(2):
        a_copy(side, 0).start()

    @pl.loop(1, n_chunks)
    def _(i):
        norm_chunk(i)

        @pl.when(i < AHEAD)
        def _():
            for side in range(2):
                a_copy(side, i).start()

    @pl.loop(0, n_w)
    def _(j):
        w_copy(j).wait()

    def finish_block(y, head, src, slot, blk):
        y = y + bqkv[head]
        t = pl.ds(pl.multiple_of(src * tok, tok), tok)
        cc, cl, cr = tab_c[t][None], tab_l[t][None], tab_r[t][None]
        for m in range(3):
            u = y[:, m * hd:(m + 1) * hd]
            if m < 2:
                far = pltpu.roll(u, hd - hd // 8, 1).reshape(PC, tok, hd)
                near = pltpu.roll(u, hd // 8, 1).reshape(PC, tok, hd)
                u = u.reshape(PC, tok, hd) * cc + far * cl + near * cr
            else:
                u = u.reshape(PC, tok, hd)
            st[slot, blk, m] = u.astype(jnp.bfloat16)

    def place(m, i, src):
        return outs[m].at[pl.ds(i * PC, PC), 0, pl.ds(pl.multiple_of(src * tok, tok), tok)]

    def send_block(i, src, slot, blk, dest):
        for m in range(3):
            pltpu.make_async_remote_copy(
                src_ref=st.at[slot, blk, m], dst_ref=place(m, i, src), send_sem=st_sem.at[slot], recv_sem=r_sem.at[m, i],
                device_id={'sp': dest}, device_id_type=MESH).start()

    n_remote = 2 * n_far + 3

    def free_slot(slot):
        pltpu.make_async_copy(st.at[slot, pl.ds(0, n_remote)], st.at[slot, pl.ds(0, n_remote)], st_sem.at[slot]).wait()
        pltpu.make_async_copy(st.at[slot, pl.ds(0, 3)], st.at[slot, pl.ds(0, 3)], self_sem.at[slot]).wait()

    def mlp_block(j):
        slot = lax.rem(j, 2)
        up_copy(j, slot).wait()
        dn_copy(j, slot).wait()
        mp = 4 * PC

        @pl.loop(0, n_prompts // mp)
        def _(r):
            rr = pl.ds(pl.multiple_of(r * mp * tok, mp * tok), mp * tok)
            x = m_buf[pl.ds(r * mp, mp)].reshape(mp * tok, d_model)
            pre = jnp.dot(x, wup_b[slot], preferred_element_type=jnp.float32) + bup[j]
            act = (0.5 * pre * (1.0 + lax.erf(pre * np.float32(np.sqrt(0.5))))).astype(jnp.bfloat16)
            acc[rr] += jnp.dot(act, wdn_b[slot], preferred_element_type=jnp.float32)

        @pl.when(j + 2 < n_fb)
        def _():
            up_copy(j + 2, slot).start()
            dn_copy(j + 2, slot).start()

    below = lax.rem(me + n - 2, n)
    above = lax.rem(me + 2, n)
    per_tick = n_fb // n_chunks

    @pl.loop(0, n_chunks)
    def _(i):
        slot = lax.rem(i, 2)
        r = pl.ds(pl.multiple_of(i * rows, rows), rows)

        @pl.when(i + AHEAD < n_chunks)
        def _():
            for side in range(2):
                a_copy(side, i + AHEAD).start()

        for side in range(2):
            a_copy(side, i).wait_recv()

        @pl.when(i >= 2)
        def _():
            free_slot(slot)

        @pl.loop(0, n_far)
        def _(t):
            jl = n_w - 1 - t
            hl = lax.rem(2 * chip - n_far + jl + n, n)
            y = jnp.dot(a_nb[0, r], w_sc[jl], preferred_element_type=jnp.float32)
            finish_block(y, hl, below, slot, t)
            send_block(i, below, slot, t, hl)
            hr = lax.rem(2 * chip - n_far + t + n, n)
            y = jnp.dot(a_nb[1, r], w_sc[t], preferred_element_type=jnp.float32)
            finish_block(y, hr, above, slot, n_far + t)
            send_block(i, above, slot, n_far + t, hr)

        @pl.loop(0, 2)
        def _(q):
            dest = 2 * chip + jnp.where(q == 1, lax.rem(me, 2), 1 - lax.rem(me, 2))
            j = dest - 2 * chip + n_far
            for g, src in enumerate((below, me, above)):
                rows_in = a_own[r] if g == 1 else a_nb[g // 2, r]
                y = jnp.dot(rows_in, w_sc[j], preferred_element_type=jnp.float32)
                finish_block(y, dest, src, slot, 2 * n_far + 3 * q + g)

            @pl.when(q == 0)
            def _():
                for g, src in enumerate((below, me, above)):
                    send_block(i, src, slot, 2 * n_far + g, dest)

            @pl.when(q == 1)
            def _():
                for g, src in enumerate((below, me, above)):
                    for m in range(3):
                        pltpu.make_async_copy(st.at[slot, n_remote + g, m], place(m, i, src), self_sem.at[slot]).start()

        @pl.loop(0, per_tick)
        def _(j):
            mlp_block(i * per_tick + j)

    out_copy = pltpu.make_async_copy(acc, acc_out, o_sem)
    out_copy.start()

    for slot in range(2):
        free_slot(slot)

    @pl.loop(0, n_chunks)
    def _(i):
        for side in range(2):
            a_copy(side, i).wait_send()
        for m in range(3):
            got = outs[m].at[pl.ds(0, PC), 0, pl.ds(0, (n - 3) * tok)]
            pltpu.make_async_copy(got, got, r_sem.at[m, i]).wait()

    out_copy.wait()


def attend_kernel(n, lens, q_in, k_in, v_in, acc_in, wout, out,
                  qb, kb, vb, ctx_st, ctx_rv, w_b, acc, out_b,
                  in_sem, w_sem, acc_sem, send_sem, recv_sem, o_sem):
    me = lax.axis_index('sp')
    n_prompts, tok, d_model = out.shape
    seq, hd = q_in.shape[2], q_in.shape[3]
    n_chunks = n_prompts // PC
    rows = PC * tok
    scale = np.float32(hd ** -0.5)

    await_barrier = entry_barrier(n, me)

    def loads(i, slot):
        return [pltpu.make_async_copy(src.at[pl.ds(i * PC, PC), 0], dst.at[slot], in_sem.at[t, slot])
                for t, (src, dst) in enumerate(((q_in, qb), (k_in, kb), (v_in, vb)))]

    for i in range(2):
        for c in loads(i, i):
            c.start()
    w_copy = pltpu.make_async_copy(wout, w_b, w_sem)
    w_copy.start()
    acc_copy = pltpu.make_async_copy(acc_in, acc, acc_sem)
    acc_copy.start()
    await_barrier()

    blk = seq // 2

    @pl.loop(0, n_chunks)
    def _(i):
        slot = lax.rem(i, 2)
        for c in loads(i, slot):
            c.wait()

        @pl.loop(0, PC)
        def _(p):
            length = lens[i * PC + p]
            for b in range(2):
                keys = (b + 1) * blk
                q = qb[slot, p, b * blk:keys]
                k = kb[slot, p, :keys]
                v = vb[slot, p, :keys]
                s = lax.dot_general(q, k, (((1,), (1,)), ((), ())), preferred_element_type=jnp.float32) * scale
                key = lax.broadcasted_iota(jnp.int32, (blk, keys), 1)
                row = lax.broadcasted_iota(jnp.int32, (blk, keys), 0) + b * blk
                s = jnp.where((key <= row) & (key < length), s, -jnp.inf)
                w = jnp.exp(s - jnp.max(s, axis=-1, keepdims=True))
                z = jnp.sum(w, axis=-1, keepdims=True)
                c = jnp.dot(w.astype(jnp.bfloat16), v, preferred_element_type=jnp.float32) / z
                ctx_st[i * PC + p, b * blk:keys] = c.astype(jnp.bfloat16)

        @pl.when(i + 2 < n_chunks)
        def _():
            for c in loads(i + 2, slot):
                c.start()

        pr = pl.ds(i * PC, PC)
        for d in range(1, n):
            dest = lax.rem(me + d, n)
            pltpu.make_async_remote_copy(
                src_ref=ctx_st.at[pr, pl.ds(pl.multiple_of(dest * tok, tok), tok)], dst_ref=ctx_rv.at[me, pr],
                send_sem=send_sem, recv_sem=recv_sem.at[i], device_id={'sp': dest}, device_id_type=MESH).start()
        ctx_rv[me, pr] = ctx_st[pr, pl.ds(pl.multiple_of(me * tok, tok), tok)]

    w_copy.wait()
    acc_copy.wait()

    def store(i, slot):
        return pltpu.make_async_copy(out_b.at[slot], out.at[pl.ds(i * PC, PC)], o_sem.at[slot])

    @pl.loop(0, n_chunks)
    def _(i):
        slot = lax.rem(i, 2)
        pr = pl.ds(i * PC, PC)
        got = ctx_rv.at[pl.ds(0, n - 1), pl.ds(0, PC)]
        pltpu.make_async_copy(got, got, recv_sem.at[i]).wait()

        @pl.when(i >= 2)
        def _():
            store(i - 2, slot).wait()

        ctx = jnp.concatenate([ctx_rv[h, pr].reshape(rows, hd) for h in range(n)], axis=1)
        r = pl.ds(pl.multiple_of(i * rows, rows), rows)
        for t in range(4):
            cols = slice(t * (d_model // 4), (t + 1) * (d_model // 4))
            y = jnp.dot(ctx, w_b[:, cols], preferred_element_type=jnp.float32) + acc[r, cols]
            out_b[slot, :, :, cols] = y.astype(jnp.bfloat16).reshape(PC, tok, d_model // 4)
        store(i, slot).start()

    for i in range(2):
        store(n_chunks - 2 + i, (n_chunks + i) % 2).wait()
    sent = ctx_st.at[:, pl.ds(0, (n - 1) * tok)]
    pltpu.make_async_copy(sent, sent, send_sem).wait()


def solution(mesh):
    n = mesh.shape['sp']
    row_spec = P('dp', 'sp', None)
    cache_spec = P('dp', 'sp', None, None)
    vec_spec = P(None)
    mat_spec = P(None, None)

    def local_layer(hidden, seq_lens, ln1_gain, ln1_bias, ln2_gain, ln2_bias, w_qkv, b_qkv, w_out, b_out, w_up, b_up, w_down, b_down):
        n_prompts, tok, d_model = hidden.shape
        n_heads, _, hd = b_qkv.shape
        d_ff = w_up.shape[1]
        seq = tok * n
        n_rows = n_prompts * tok
        n_chunks = n_prompts // PC
        rows = PC * tok
        fb = min(FB, d_ff // n_chunks)
        n_far = n // 2 - 3
        bf, f32 = jnp.bfloat16, jnp.float32
        row = lambda v: v.reshape(1, d_model)
        tabs = [jnp.asarray(t) for t in rotary_tables(seq, hd)]
        cache = jax.ShapeDtypeStruct((n_prompts, 1, seq, hd), bf)
        dma = pltpu.SemaphoreType.DMA
        q, k, v, acc = pl.pallas_call(
            functools.partial(project_kernel, n),
            name='project',
            out_shape=(cache, cache, cache, jax.ShapeDtypeStruct((n_rows, d_model), f32)),
            in_specs=[ANY, VM, VM, VM, VM, ANY, VM, VM, VM, VM, ANY, VM, ANY, VM],
            out_specs=(ANY, ANY, ANY, ANY),
            scratch_shapes=[
                pltpu.VMEM((n_rows, d_model), bf),
                pltpu.VMEM((2, n_rows, d_model), bf),
                pltpu.VMEM((n_prompts, tok, d_model), bf),
                pltpu.VMEM((n_rows, d_model), f32),
                pltpu.VMEM((2 * n_far + 2, d_model, 3 * hd), bf),
                pltpu.VMEM((2, d_model, fb), bf),
                pltpu.VMEM((2, fb, d_model), bf),
                pltpu.VMEM((2, 2 * n_far + 6, 3, PC, tok, hd), bf),
                dma((n_chunks,)), dma((2 * n_far + 2,)), dma((2,)), dma((2,)), dma((2, n_chunks)), dma((2, n_chunks)),
                dma((2,)), dma((2,)), dma((3, n_chunks)), dma(()),
            ],
            compiler_params=pltpu.CompilerParams(collective_id=0, has_side_effects=True, vmem_limit_bytes=VMEM_LIMIT),
            cost_estimate=pl.CostEstimate(flops=2 * n_rows * d_model * (3 * d_model + 2 * d_ff), bytes_accessed=200_000_000, transcendentals=0),
        )(hidden, row(ln1_gain), row(ln1_bias), row(ln2_gain), row(ln2_bias), w_qkv, b_qkv.reshape(n_heads, 1, 3 * hd), *tabs,
          w_up, b_up.reshape(d_ff // fb, 1, fb), w_down, row(b_out + b_down))
        out = pl.pallas_call(
            functools.partial(attend_kernel, n),
            name='attend',
            out_shape=jax.ShapeDtypeStruct((n_prompts, tok, d_model), bf),
            in_specs=[SM, ANY, ANY, ANY, ANY, ANY],
            out_specs=ANY,
            scratch_shapes=[
                pltpu.VMEM((2, PC, seq, hd), bf), pltpu.VMEM((2, PC, seq, hd), bf), pltpu.VMEM((2, PC, seq, hd), bf),
                pltpu.VMEM((n_prompts, seq, hd), bf),
                pltpu.VMEM((n, n_prompts, tok, hd), bf),
                pltpu.VMEM((d_model, d_model), bf),
                pltpu.VMEM((n_rows, d_model), f32),
                pltpu.VMEM((2, PC, tok, d_model), bf),
                dma((3, 2)), dma(()), dma(()), dma(()), dma((n_chunks,)), dma((2,)),
            ],
            compiler_params=pltpu.CompilerParams(collective_id=1, has_side_effects=True, vmem_limit_bytes=VMEM_LIMIT),
            cost_estimate=pl.CostEstimate(flops=2 * n_rows * d_model * d_model, bytes_accessed=50_000_000, transcendentals=0),
        )(seq_lens, q, k, v, acc, w_out)
        return out, k, v

    return jax.shard_map(local_layer, mesh=mesh,
                         in_specs=(row_spec, P('dp'), vec_spec, vec_spec, vec_spec, vec_spec, mat_spec, P(None, None, None), mat_spec, vec_spec, mat_spec, vec_spec, mat_spec, vec_spec),
                         out_specs=(row_spec, cache_spec, cache_spec), check_vma=False)
```

time: 918 us -> 376 us (0.41)
  Pallas kernels: 0 us -> 358 us
  matrix products: 325 us -> 0 us
  waiting for transfers between devices: 280 us -> 0 us
  other arithmetic: 141 us -> 1.31 us
  local copies, waits for them, and re-layouts: 115 us -> 12 us
  loops' own time: 26.8 us -> 0 us
  starting transfers between devices: 17.5 us -> 0 us
    pallas_call x0 -> x2, Pallas kernels: none -> 358 us  [the longest x1 256 us: local_layer(): pl.pallas_call(functools.partial(project_kernel, n), name='project', out_...]
    dot_general x36 -> x0, matrix products: 325 us -> none  [the longest x1 109 us: local_layer(): jnp.dot(mlp_in.reshape(n_prompts * rows_dev, d_model), w_up, preferred_el...]
    all_to_all x2 -> x0, waiting for transfers between devices: 280 us -> none  [the longest x1 280 us: local_layer(): by_heads = lax.all_to_all(packed, 'sp', 2, 1, tiled=True)]
    another operation x2 -> x0, other arithmetic: 57.4 us -> none
    concatenate x1 -> x0, other arithmetic: 50.5 us -> none  [local_layer(): jnp.concatenate([rotated, proj_qkv[:, :, :, 2:]], axis=3)]
    reshape x1, local copies, waits for them, and re-layouts: 40.9 us -> 0.64 us  [local_layer(): b_qkv.reshape(n_heads, 1, 3 * hd)]
    another operation x1 -> x0, loops' own time: 26.8 us -> none  [local_layer(): ctx_blocks = lax.map(one_block, jnp.arange(n_shards) * rows_dev)]
    slice x2 -> x0, local copies, waits for them, and re-layouts: 23.2 us -> none  [the longest x1 12.7 us: rotary(): vecs[..., 2 * half_rot:]]
  transfers between devices with their start and end apart: 2 -> 0, of which waited for: 1 -> 0; matrix products, arithmetic and copies ran while one was open for 13% -> 0% of each run, Pallas kernels for 0% -> 0%
where the time goes in v1:
time: 376 us; the launch traced here: 372 us
  Pallas kernels  358 us (95%)
  local copies, waits for them, and re-layouts  12 us (3%)
    pallas_call x1, Pallas kernels, local_layer(): pl.pallas_call(functools.partial(project_kernel, n), name='project', out_...  256 us
    pallas_call x1, Pallas kernels, local_layer(): pl.pallas_call(functools.partial(attend_kernel, n), name='attend', out_sh...  102 us
    unnamed x8, local copies, waits for them, and re-layouts  11.4 us

profile of v1, /device:TPU:21, one launch (start us, length us, event | category | flops | bytes accessed | tf_op | source)
XLA Modules:
  0.0 372.2 jit_solution(17838128189613805643)
XLA Ops:
  0.6 1.3 add.3
  1.9 0.8 copy.21
  2.7 0.6 reshape.34.bqkv
  3.3 255.8 %project.1 = (bf16[32,1,512,128]{3,2,1,0:T(8,128)(2,1)}, bf16[32,1,512,128]{3,2,1,0:T(8,128)(2,1)}, bf16[32,1,512,128]{3,2,1,0:T(8,128)(2,1)}, f32[1024,2048]{1,0:T(8,128)}) custom-call(bf16[32,32,2048]{2,1,0:T(8,128)(2,1)} %hid.1, f32[1,2048]{1,0:T(1,128)} %bitcast.8, f32[1,2048]{1,0:T(1,128)} %bitcast.9, f32[1,2048]{1,0:T(1,128)} %bitcast.10, ...), custom_call_target="tpu_custom_call" | custom-call | flops 94489280512 | bytes 200000000 | tf_op jit(solution)/shard_map/project/pallas_call | solution.py:366
  259.2 102.3 %attend.1 = bf16[32,32,2048]{2,1,0:T(8,128)(2,1)} custom-call(s32[32]{0:T(128)} %lens.1, bf16[32,1,512,128]{3,2,1,0:T(8,128)(2,1)} %get-tuple-element.7.q_in, bf16[32,1,512,128]{3,2,1,0:T(8,128)(2,1)} %get-tuple-element.15.k_in, bf16[32,1,512,128]{3,2,1,0:T(8,128)(2,1)} %get-tuple-element.16.v_in, f32[1024,2048]{1,0:T(8,128)} %get-tuple-element.10.acc_in, ...), custom_call_target="tpu_custom_call" | custom-call | flops 8589934592 | bytes 50000000 | tf_op jit(solution)/shard_map/attend/pallas_call | solution.py:388
  361.5 0.0 copy-start.1
  361.5 4.9 %copy.26 = bf16[32,32,2048]{2,1,0:T(8,128)(2,1)} copy(bf16[32,32,2048]{2,1,0:T(8,128)(2,1)} %attend.1) | data formatting | bytes 8388608
  366.5 0.0 copy-done.1
  366.5 0.0 copy-start
  366.5 2.1 copy.27
  368.6 1.6 copy-done
  370.2 2.0 copy.28
Async XLA Ops:
  361.5 5.0 %copy-start.1 = (bf16[32,1,512,128]{3,2,1,0:T(8,128)(2,1)S(1)}, bf16[32,1,512,128]{3,2,1,0:T(8,128)(2,1)}, u32[]{:S(2)}) copy-start(bf16[32,1,512,128]{3,2,1,0:T(8,128)(2,1)} %get-tuple-element.15.k_in) | copy-start | bytes 12582916
  366.5 3.7 copy-start

commit v2 on v1

v2 whole, which is shorter than its diff:
```python
import functools

import jax
import jax.numpy as jnp
import numpy as np
from jax import lax
from jax.experimental import pallas as pl
from jax.experimental.pallas import tpu as pltpu
from jax.sharding import PartitionSpec as P

LN_EPS = 1e-5
ROT_BASE = 10000.0
PC = 4
AHEAD = 3
FB = 256
MESH = pl.DeviceIdType.MESH
VMEM_LIMIT = 66_900_000
ANY = pl.BlockSpec(memory_space=pl.ANY)
VM = pl.BlockSpec(memory_space=pltpu.VMEM)
SM = pl.BlockSpec(memory_space=pltpu.SMEM)


def rotary_tables(seq_len, head_dim):
    rot = head_dim // 4
    half = rot // 2
    inv = np.float32(ROT_BASE) ** (np.float32(-2.0) * np.arange(half, dtype=np.float32) / np.float32(rot))
    ang = np.arange(seq_len, dtype=np.float32)[:, None] * inv[None, :].astype(np.float32)
    cos, sin = np.cos(ang), np.sin(ang)
    c = np.ones((seq_len, head_dim), np.float32)
    s = np.zeros((2, seq_len, head_dim), np.float32)
    c[:, :half] = cos
    c[:, half:rot] = cos
    s[0, :, :half] = -sin
    s[1, :, half:rot] = sin
    return c, s[0], s[1]


def entry_barrier(n, me):
    sem = pltpu.get_barrier_semaphore()
    for d in range(1, n):
        pl.semaphore_signal(sem, inc=1, device_id={'sp': lax.rem(me + d, n)}, device_id_type=MESH)
    return lambda: pl.semaphore_wait(sem, n - 1)


def layer_kernel(n, lens, hid, g1, s1, g2, s2, wqkv, bqkv, tab_c, tab_l, tab_r, wup, bup, wdn, bdn, wout, bout,
                 q_out, k_out, v_out, out,
                 a_own, a_nb, m_buf, acc, w_sc, wup_b, wdn_b, st, qb, kb, vb, ctx_st, ctx_rv, out_b,
                 x_sem, w_sem, up_sem, dn_sem, a_send, a_recv, st_sem, self_sem, r_sem, in_sem, c_send, c_recv, wo_sem, o_sem):
    me = lax.axis_index('sp')
    chip = lax.div(me, 2)
    n_prompts, tok, d_model = hid.shape
    seq, hd = q_out.shape[2], q_out.shape[3]
    wide = 3 * hd
    n_chunks = n_prompts // PC
    rows = PC * tok
    n_far = n // 2 - 3
    n_w = 2 * n_far + 2
    n_remote = 2 * n_far + 3
    n_fb, fb = bup.shape[0], bup.shape[2]
    per_tick = n_fb // n_chunks
    outs = (q_out, k_out, v_out)
    scale = np.float32(hd ** -0.5)
    below = lax.rem(me + n - 2, n)
    above = lax.rem(me + 2, n)

    await_barrier = entry_barrier(n, me)

    def chunk_rows(i):
        return pl.ds(pl.multiple_of(i * rows, rows), rows)

    def chunk(i):
        return pl.ds(i * PC, PC)

    def tokens_of(s):
        return pl.ds(pl.multiple_of(s * tok, tok), tok)

    def await_bytes(ref, sem):
        pltpu.make_async_copy(ref, ref, sem).wait()

    def x_copy(i):
        return pltpu.make_async_copy(hid.at[chunk(i)], m_buf.at[chunk(i)], x_sem.at[i])

    def head_at(j):
        return lax.rem(2 * chip - n_far + j + n, n)

    def w_copy(j):
        cols = pl.ds(pl.multiple_of(head_at(j) * wide, 128), wide)
        return pltpu.make_async_copy(wqkv.at[:, cols], w_sc.at[j], w_sem.at[j])

    def up_copy(j, slot):
        return pltpu.make_async_copy(wup.at[:, pl.ds(pl.multiple_of(j * fb, 128), fb)], wup_b.at[slot], up_sem.at[slot])

    def dn_copy(j, slot):
        return pltpu.make_async_copy(wdn.at[pl.ds(pl.multiple_of(j * fb, 128), fb)], wdn_b.at[slot], dn_sem.at[slot])

    @pl.loop(0, n_chunks)
    def _(i):
        x_copy(i).start()

    @pl.loop(0, n_w)
    def _(j):
        w_copy(j).start()

    for j in range(2):
        up_copy(j, j).start()
        dn_copy(j, j).start()

    def a_copy(side, i):
        return pltpu.make_async_remote_copy(
            src_ref=a_own.at[chunk_rows(i)], dst_ref=a_nb.at[side, chunk_rows(i)], send_sem=a_send.at[side, i],
            recv_sem=a_recv.at[side, i], device_id={'sp': above if side == 0 else below}, device_id_type=MESH)

    def norm_chunk(i):
        x_copy(i).wait()
        x = m_buf[chunk(i)].reshape(rows, d_model).astype(jnp.float32)
        cen = x - jnp.mean(x, axis=-1, keepdims=True)
        var = jnp.mean(cen * cen, axis=-1, keepdims=True)
        nor = cen * lax.rsqrt(var + LN_EPS)
        a_own[chunk_rows(i)] = (nor * g1[...] + s1[...]).astype(jnp.bfloat16)
        m_buf[chunk(i)] = (nor * g2[...] + s2[...]).astype(jnp.bfloat16).reshape(PC, tok, d_model)
        acc[chunk_rows(i)] = x + (bout[...] + bdn[...])

    norm_chunk(0)
    await_barrier()
    for side in range(2):
        a_copy(side, 0).start()

    @pl.loop(1, n_chunks)
    def _(i):
        norm_chunk(i)

        @pl.when(i < AHEAD)
        def _():
            for side in range(2):
                a_copy(side, i).start()

    @pl.loop(0, n_w)
    def _(j):
        w_copy(j).wait()

    def finish_block(y, head, src, slot, blk):
        t = tokens_of(src)
        cc, cl, cr = tab_c[t][None], tab_l[t][None], tab_r[t][None]
        for m in range(3):
            u = y[:, m * hd:(m + 1) * hd] + bqkv[m, pl.ds(head, 1)]
            if m < 2:
                far = pltpu.roll(u, hd - hd // 8, 1).reshape(PC, tok, hd)
                near = pltpu.roll(u, hd // 8, 1).reshape(PC, tok, hd)
                u = u.reshape(PC, tok, hd) * cc + far * cl + near * cr
            else:
                u = u.reshape(PC, tok, hd)
            st[slot, blk, m] = u.astype(jnp.bfloat16)

    def place(m, i, src):
        return outs[m].at[chunk(i), 0, tokens_of(src)]

    def send_block(i, src, slot, blk, dest):
        for m in range(3):
            pltpu.make_async_remote_copy(
                src_ref=st.at[slot, blk, m], dst_ref=place(m, i, src), send_sem=st_sem.at[slot], recv_sem=r_sem.at[m, i],
                device_id={'sp': dest}, device_id_type=MESH).start()

    def free_slot(slot):
        await_bytes(st.at[slot, pl.ds(0, n_remote)], st_sem.at[slot])
        await_bytes(st.at[slot, pl.ds(0, 3)], self_sem.at[slot])

    def project_chunk(i):
        slot = lax.rem(i, 2)
        r = chunk_rows(i)

        for side in range(2):
            a_copy(side, i).wait_recv()

        @pl.loop(0, n_far)
        def _(t):
            jl = n_w - 1 - t
            y = jnp.dot(a_nb[0, r], w_sc[jl], preferred_element_type=jnp.float32)
            finish_block(y, head_at(jl), below, slot, t)
            send_block(i, below, slot, t, head_at(jl))
            y = jnp.dot(a_nb[1, r], w_sc[t], preferred_element_type=jnp.float32)
            finish_block(y, head_at(t), above, slot, n_far + t)
            send_block(i, above, slot, n_far + t, head_at(t))

        @pl.loop(0, 2)
        def _(q):
            dest = 2 * chip + jnp.where(q == 1, lax.rem(me, 2), 1 - lax.rem(me, 2))
            j = dest - 2 * chip + n_far
            for g, src in enumerate((below, me, above)):
                rows_in = a_own[r] if g == 1 else a_nb[g // 2, r]
                y = jnp.dot(rows_in, w_sc[j], preferred_element_type=jnp.float32)
                finish_block(y, dest, src, slot, 2 * n_far + 3 * q + g)

            @pl.when(q == 0)
            def _():
                for g, src in enumerate((below, me, above)):
                    send_block(i, src, slot, 2 * n_far + g, dest)

            @pl.when(q == 1)
            def _():
                for g, src in enumerate((below, me, above)):
                    for m in range(3):
                        pltpu.make_async_copy(st.at[slot, n_remote + g, m], place(m, i, src), self_sem.at[slot]).start()

    def mlp_block(j):
        slot = lax.rem(j, 2)
        up_copy(j, slot).wait()
        dn_copy(j, slot).wait()
        mp = 2 * PC

        @pl.loop(0, n_prompts // mp)
        def _(r):
            rr = pl.ds(pl.multiple_of(r * mp * tok, mp * tok), mp * tok)
            x = m_buf[pl.ds(r * mp, mp)].reshape(mp * tok, d_model)
            pre = jnp.dot(x, wup_b[slot], preferred_element_type=jnp.float32) + bup[j]
            act = (0.5 * pre * (1.0 + lax.erf(pre * np.float32(np.sqrt(0.5))))).astype(jnp.bfloat16)
            acc[rr] += jnp.dot(act, wdn_b[slot], preferred_element_type=jnp.float32)

        @pl.when(j + 2 < n_fb)
        def _():
            up_copy(j + 2, slot).start()
            dn_copy(j + 2, slot).start()

    blk = seq // 2

    def attend_chunk(i):
        slot = lax.rem(i, 2)
        loads = []
        for m, dst in enumerate((qb, kb, vb)):
            await_bytes(outs[m].at[chunk(0), 0, pl.ds(0, (n - 3) * tok)], r_sem.at[m, i])
            loads.append(pltpu.make_async_copy(outs[m].at[chunk(i), 0], dst, in_sem.at[m]))
            loads[-1].start()

        @pl.when(i >= 2)
        def _():
            await_bytes(ctx_st.at[slot, :, pl.ds(0, (n - 1) * tok)], c_send.at[slot])

        for c in loads:
            c.wait()

        @pl.loop(0, PC)
        def _(p):
            length = lens[i * PC + p]
            for b in range(2):
                keys = (b + 1) * blk
                s = lax.dot_general(qb[p, b * blk:keys], kb[p, :keys], (((1,), (1,)), ((), ())),
                                    preferred_element_type=jnp.float32) * scale
                key = lax.broadcasted_iota(jnp.int32, (blk, keys), 1)
                row = lax.broadcasted_iota(jnp.int32, (blk, keys), 0) + b * blk
                s = jnp.where((key <= row) & (key < length), s, -jnp.inf)
                w = jnp.exp(s - jnp.max(s, axis=-1, keepdims=True))
                z = jnp.sum(w, axis=-1, keepdims=True)
                c = jnp.dot(w.astype(jnp.bfloat16), vb[p, :keys], preferred_element_type=jnp.float32) / z
                ctx_st[slot, p, b * blk:keys] = c.astype(jnp.bfloat16)

        for d in range(1, n):
            dest = lax.rem(me + d, n)
            pltpu.make_async_remote_copy(
                src_ref=ctx_st.at[slot, :, tokens_of(dest)], dst_ref=ctx_rv.at[me, chunk(i)], send_sem=c_send.at[slot],
                recv_sem=c_recv.at[i], device_id={'sp': dest}, device_id_type=MESH).start()
        ctx_rv[me, chunk(i)] = ctx_st[slot, :, tokens_of(me)]

    half = wout.shape[0] // 2
    wo_copies = [pltpu.make_async_copy(wout.at[pl.ds(k * half, half)], a_nb.at[k, pl.ds(0, half)], wo_sem.at[k]) for k in range(2)]

    def store(i, slot):
        return pltpu.make_async_copy(out_b.at[slot], out.at[chunk(i)], o_sem.at[slot])

    def finish_chunk(i):
        slot = lax.rem(i, 2)
        await_bytes(ctx_rv.at[pl.ds(0, n - 1), chunk(0)], c_recv.at[i])

        @pl.when(i >= 2)
        def _():
            store(i - 2, slot).wait()

        width = d_model // 4
        ctx = [jnp.concatenate([ctx_rv[k * (n // 2) + h, chunk(i)].reshape(rows, hd) for h in range(n // 2)], axis=1) for k in range(2)]
        for t in range(4):
            cols = slice(t * width, (t + 1) * width)
            y = acc[chunk_rows(i), cols]
            for k in range(2):
                y = y + jnp.dot(ctx[k], a_nb[k, :half, cols], preferred_element_type=jnp.float32)
            out_b[slot, :, :, cols] = y.astype(jnp.bfloat16).reshape(PC, tok, width)
        store(i, slot).start()

    @pl.loop(0, n_chunks + 2)
    def _(i):
        @pl.when(i + AHEAD < n_chunks)
        def _():
            for side in range(2):
                a_copy(side, i + AHEAD).start()

        @pl.when(i >= 2)
        def _():
            free_slot(lax.rem(i, 2))

        @pl.when(i < n_chunks)
        def _():
            project_chunk(i)

            @pl.when(i == n_chunks - 1)
            def _():
                for c in wo_copies:
                    c.start()

            @pl.loop(0, per_tick)
            def _(j):
                mlp_block(i * per_tick + j)

        @pl.when(i >= 2)
        def _():
            attend_chunk(i - 2)

        @pl.when(i == n_chunks)
        def _():
            for c in wo_copies:
                c.wait()

            @pl.loop(0, n_chunks - 3)
            def _(j):
                finish_chunk(j)

    @pl.loop(n_chunks - 3, n_chunks)
    def _(j):
        finish_chunk(j)

    for slot in range(2):
        await_bytes(ctx_st.at[slot, :, pl.ds(0, (n - 1) * tok)], c_send.at[slot])
        store(n_chunks - 2 + slot, (n_chunks + slot) % 2).wait()

    @pl.loop(0, n_chunks)
    def _(i):
        for side in range(2):
            a_copy(side, i).wait_send()


def hand_on_kernel(a, b, c, a_out, b_out, c_out, a_v, b_v, c_v, in_sem, out_sem):
    parts = in_sem.shape[1]
    size = a.shape[0] // parts
    trio = ((a, a_v, a_out), (b, b_v, b_out), (c, c_v, c_out))

    def copies(t, p):
        src, mid, dst = trio[t]
        s = pl.ds(p * size, size)
        return (pltpu.make_async_copy(src.at[s], mid.at[s], in_sem.at[t, p]),
                pltpu.make_async_copy(mid.at[s], dst.at[s], out_sem.at[t, p]))

    steps = [(t, p) for p in range(parts) for t in range(3)]
    for s in steps:
        copies(*s)[0].start()
    for s in steps:
        copies(*s)[0].wait()
        copies(*s)[1].start()
    for s in steps:
        copies(*s)[1].wait()


def solution(mesh):
    n = mesh.shape['sp']
    row_spec = P('dp', 'sp', None)
    cache_spec = P('dp', 'sp', None, None)
    vec_spec = P(None)
    mat_spec = P(None, None)

    def local_layer(hidden, seq_lens, ln1_gain, ln1_bias, ln2_gain, ln2_bias, w_qkv, b_qkv, w_out, b_out, w_up, b_up, w_down, b_down):
        n_prompts, tok, d_model = hidden.shape
        hd = b_qkv.shape[2]
        d_ff = w_up.shape[1]
        seq = tok * n
        n_rows = n_prompts * tok
        n_chunks = n_prompts // PC
        fb = min(FB, d_ff // n_chunks)
        n_far = n // 2 - 3
        bf, f32 = jnp.bfloat16, jnp.float32
        row = lambda v: v.reshape(1, d_model)
        tabs = [jnp.asarray(t) for t in rotary_tables(seq, hd)]
        cache = jax.ShapeDtypeStruct((n_prompts, 1, seq, hd), bf)
        like_out = jax.ShapeDtypeStruct((n_prompts, tok, d_model), bf)
        dma = pltpu.SemaphoreType.DMA
        q, k, v, out = pl.pallas_call(
            functools.partial(layer_kernel, n),
            name='layer',
            out_shape=(cache, cache, cache, like_out),
            in_specs=[SM, ANY, VM, VM, VM, VM, ANY, VM, VM, VM, VM, ANY, VM, ANY, VM, ANY, VM],
            out_specs=(ANY, ANY, ANY, ANY),
            scratch_shapes=[
                pltpu.VMEM((n_rows, d_model), bf),
                pltpu.VMEM((2, max(n_rows, w_out.shape[0] // 2), d_model), bf),
                pltpu.VMEM((n_prompts, tok, d_model), bf),
                pltpu.VMEM((n_rows, d_model), f32),
                pltpu.VMEM((2 * n_far + 2, d_model, 3 * hd), bf),
                pltpu.VMEM((2, d_model, fb), bf),
                pltpu.VMEM((2, fb, d_model), bf),
                pltpu.VMEM((2, 2 * n_far + 6, 3, PC, tok, hd), bf),
                pltpu.VMEM((PC, seq, hd), bf), pltpu.VMEM((PC, seq, hd), bf), pltpu.VMEM((PC, seq, hd), bf),
                pltpu.VMEM((2, PC, seq, hd), bf),
                pltpu.VMEM((n, n_prompts, tok, hd), bf),
                pltpu.VMEM((2, PC, tok, d_model), bf),
                dma((n_chunks,)), dma((2 * n_far + 2,)), dma((2,)), dma((2,)), dma((2, n_chunks)), dma((2, n_chunks)),
                dma((2,)), dma((2,)), dma((3, n_chunks)), dma((3,)), dma((2,)), dma((n_chunks,)), dma((2,)), dma((2,)),
            ],
            compiler_params=pltpu.CompilerParams(collective_id=0, has_side_effects=True, vmem_limit_bytes=VMEM_LIMIT),
            cost_estimate=pl.CostEstimate(flops=2 * n_rows * d_model * (4 * d_model + 2 * d_ff), bytes_accessed=200_000_000, transcendentals=0),
        )(seq_lens, hidden, row(ln1_gain), row(ln1_bias), row(ln2_gain), row(ln2_bias), w_qkv, jnp.transpose(b_qkv, (1, 0, 2)), *tabs,
          w_up, b_up.reshape(d_ff // fb, 1, fb), w_down, row(b_down), w_out, row(b_out))
        parts = 4
        return pl.pallas_call(
            hand_on_kernel,
            name='hand_on',
            out_shape=(like_out, cache, cache),
            in_specs=[ANY] * 3,
            out_specs=(ANY,) * 3,
            scratch_shapes=[pltpu.VMEM(like_out.shape, bf), pltpu.VMEM(cache.shape, bf), pltpu.VMEM(cache.shape, bf),
                            dma((3, parts)), dma((3, parts))],
            compiler_params=pltpu.CompilerParams(vmem_limit_bytes=VMEM_LIMIT),
        )(out, k, v)

    return jax.shard_map(local_layer, mesh=mesh,
                         in_specs=(row_spec, P('dp'), vec_spec, vec_spec, vec_spec, vec_spec, mat_spec, P(None, None, None), mat_spec, vec_spec, mat_spec, vec_spec, mat_spec, vec_spec),
                         out_specs=(row_spec, cache_spec, cache_spec), check_vma=False)
```

time: 376 us -> 358 us (0.952)
  local copies, waits for them, and re-layouts: 12 us -> 0 us
    unnamed x8 -> x0, local copies, waits for them, and re-layouts: 11.4 us -> none
where the time goes in v2:
time: 358 us; the launch traced here: 356 us
  Pallas kernels  356 us (99%)
    pallas_call x1, Pallas kernels, local_layer(): pl.pallas_call(functools.partial(layer_kernel, n), name='layer', out_shap...  346 us
    pallas_call x1, Pallas kernels, local_layer(): pl.pallas_call(hand_on_kernel, name='hand_on', out_shape=(like_out, cache...  9.2 us

profile of v2, /device:TPU:21, one launch (start us, length us, event | category | flops | bytes accessed | tf_op | source)
XLA Modules:
  0.0 356.3 jit_solution(8027458016558329902)
XLA Ops:
  0.6 346.4 %layer.1 = (bf16[32,1,512,128]{3,2,1,0:T(8,128)(2,1)}, bf16[32,1,512,128]{3,2,1,0:T(8,128)(2,1)}, bf16[32,1,512,128]{3,2,1,0:T(8,128)(2,1)}, bf16[32,32,2048]{2,1,0:T(8,128)(2,1)}) custom-call(s32[32]{0:T(128)} %lens.1, bf16[32,32,2048]{2,1,0:T(8,128)(2,1)} %hid.1, f32[1,2048]{1,0:T(1,128)} %bitcast.10, f32[1,2048]{1,0:T(1,128)} %bitcast.11, ...), custom_call_target="tpu_custom_call" | custom-call | flops 103079215104 | bytes 200000000 | tf_op jit(solution)/shard_map/layer/pallas_call | solution.py:380
  347.1 9.2 %hand_on.1 = (bf16[32,32,2048]{2,1,0:T(8,128)(2,1)}, bf16[32,1,512,128]{3,2,1,0:T(8,128)(2,1)}, bf16[32,1,512,128]{3,2,1,0:T(8,128)(2,1)}) custom-call(bf16[32,32,2048]{2,1,0:T(8,128)(2,1)} %get-tuple-element.6.a, bf16[32,1,512,128]{3,2,1,0:T(8,128)(2,1)} %get-tuple-element.7.b, bf16[32,1,512,128]{3,2,1,0:T(8,128)(2,1)} %get-tuple-element.8.c), custom_call_target="tpu_custom_call" | custom-call | tf_op jit(solution)/shard_map/hand_on/pallas_call | solution.py:407

commit v3 on v2

--- a/solution.py
+++ b/solution.py
@@ -12,9 +12,10 @@
 ROT_BASE = 10000.0
 PC = 4
 AHEAD = 3
-FB = 256
+FB = 512
+W_SLOTS = 4
 MESH = pl.DeviceIdType.MESH
-VMEM_LIMIT = 66_900_000
+VMEM_LIMIT = 54_400_000
 ANY = pl.BlockSpec(memory_space=pl.ANY)
 VM = pl.BlockSpec(memory_space=pltpu.VMEM)
 SM = pl.BlockSpec(memory_space=pltpu.SMEM)
@@ -44,8 +45,8 @@
 
 def layer_kernel(n, lens, hid, g1, s1, g2, s2, wqkv, bqkv, tab_c, tab_l, tab_r, wup, bup, wdn, bdn, wout, bout,
                  q_out, k_out, v_out, out,
-                 a_own, a_nb, m_buf, acc, w_sc, wup_b, wdn_b, st, qb, kb, vb, ctx_st, ctx_rv, out_b,
-                 x_sem, w_sem, up_sem, dn_sem, a_send, a_recv, st_sem, self_sem, r_sem, in_sem, c_send, c_recv, wo_sem, o_sem):
+                 a_own, a_nb, m_buf, acc, w_sc, wup_b, wdn_b, st, qb, ctx_st, ctx_rv,
+                 x_sem, w_sem, up_sem, dn_sem, a_send, a_recv, st_sem, self_sem, r_sem, in_sem, c_send, c_recv, wo_sem):
     me = lax.axis_index('sp')
     chip = lax.div(me, 2)
     n_prompts, tok, d_model = hid.shape
@@ -55,6 +56,7 @@
     rows = PC * tok
     n_far = n // 2 - 3
     n_w = 2 * n_far + 2
+    n_slots = w_sc.shape[0]
     n_remote = 2 * n_far + 3
     n_fb, fb = bup.shape[0], bup.shape[2]
     per_tick = n_fb // n_chunks
@@ -83,9 +85,19 @@
     def head_at(j):
         return lax.rem(2 * chip - n_far + j + n, n)
 
-    def w_copy(j):
+    def w_copy(k):
+        j = jnp.where(k < 2 * n_far, jnp.where(lax.rem(k, 2) == 0, n_w - 1 - lax.div(k, 2), lax.div(k, 2)),
+                      n_far + jnp.where(k == 2 * n_far, 1 - lax.rem(me, 2), lax.rem(me, 2)))
         cols = pl.ds(pl.multiple_of(head_at(j) * wide, 128), wide)
-        return pltpu.make_async_copy(wqkv.at[:, cols], w_sc.at[j], w_sem.at[j])
+        slot = lax.rem(k, n_slots)
+        return pltpu.make_async_copy(wqkv.at[:, cols], w_sc.at[slot], w_sem.at[slot])
+
+    def next_weights(i, k):
+        after = k + n_slots
+
+        @pl.when((after < n_w) | (i < n_chunks - 1))
+        def _():
+            w_copy(lax.rem(after, n_w)).start()
 
     def up_copy(j, slot):
         return pltpu.make_async_copy(wup.at[:, pl.ds(pl.multiple_of(j * fb, 128), fb)], wup_b.at[slot], up_sem.at[slot])
@@ -97,9 +109,9 @@
     def _(i):
         x_copy(i).start()
 
-    @pl.loop(0, n_w)
-    def _(j):
-        w_copy(j).start()
+    @pl.loop(0, n_slots)
+    def _(k):
+        w_copy(k).start()
 
     for j in range(2):
         up_copy(j, j).start()
@@ -133,10 +145,6 @@
         def _():
             for side in range(2):
                 a_copy(side, i).start()
-
-    @pl.loop(0, n_w)
-    def _(j):
-        w_copy(j).wait()
 
     def finish_block(y, head, src, slot, blk):
         t = tokens_of(src)
@@ -173,22 +181,24 @@
 
         @pl.loop(0, n_far)
         def _(t):
-            jl = n_w - 1 - t
-            y = jnp.dot(a_nb[0, r], w_sc[jl], preferred_element_type=jnp.float32)
-            finish_block(y, head_at(jl), below, slot, t)
-            send_block(i, below, slot, t, head_at(jl))
-            y = jnp.dot(a_nb[1, r], w_sc[t], preferred_element_type=jnp.float32)
-            finish_block(y, head_at(t), above, slot, n_far + t)
-            send_block(i, above, slot, n_far + t, head_at(t))
+            for side, (src, j) in enumerate(((below, n_w - 1 - t), (above, t))):
+                k = 2 * t + side
+                w_copy(k).wait()
+                y = jnp.dot(a_nb[side, r], w_sc[lax.rem(k, n_slots)], preferred_element_type=jnp.float32)
+                finish_block(y, head_at(j), src, slot, side * n_far + t)
+                send_block(i, src, slot, side * n_far + t, head_at(j))
+                next_weights(i, k)
 
         @pl.loop(0, 2)
         def _(q):
             dest = 2 * chip + jnp.where(q == 1, lax.rem(me, 2), 1 - lax.rem(me, 2))
-            j = dest - 2 * chip + n_far
+            k = 2 * n_far + q
+            w_copy(k).wait()
             for g, src in enumerate((below, me, above)):
                 rows_in = a_own[r] if g == 1 else a_nb[g // 2, r]
-                y = jnp.dot(rows_in, w_sc[j], preferred_element_type=jnp.float32)
+                y = jnp.dot(rows_in, w_sc[lax.rem(k, n_slots)], preferred_element_type=jnp.float32)
                 finish_block(y, dest, src, slot, 2 * n_far + 3 * q + g)
+            next_weights(i, k)
 
             @pl.when(q == 0)
             def _():
@@ -224,32 +234,30 @@
 
     def attend_chunk(i):
         slot = lax.rem(i, 2)
-        loads = []
-        for m, dst in enumerate((qb, kb, vb)):
+        for m in range(3):
             await_bytes(outs[m].at[chunk(0), 0, pl.ds(0, (n - 3) * tok)], r_sem.at[m, i])
-            loads.append(pltpu.make_async_copy(outs[m].at[chunk(i), 0], dst, in_sem.at[m]))
-            loads[-1].start()
+        q_load = pltpu.make_async_copy(q_out.at[chunk(i), 0], qb, in_sem)
+        q_load.start()
 
         @pl.when(i >= 2)
         def _():
             await_bytes(ctx_st.at[slot, :, pl.ds(0, (n - 1) * tok)], c_send.at[slot])
 
-        for c in loads:
-            c.wait()
+        q_load.wait()
 
         @pl.loop(0, PC)
         def _(p):
             length = lens[i * PC + p]
             for b in range(2):
                 keys = (b + 1) * blk
-                s = lax.dot_general(qb[p, b * blk:keys], kb[p, :keys], (((1,), (1,)), ((), ())),
+                s = lax.dot_general(qb[p, b * blk:keys], k_out[i * PC + p, 0, :keys], (((1,), (1,)), ((), ())),
                                     preferred_element_type=jnp.float32) * scale
                 key = lax.broadcasted_iota(jnp.int32, (blk, keys), 1)
                 row = lax.broadcasted_iota(jnp.int32, (blk, keys), 0) + b * blk
                 s = jnp.where((key <= row) & (key < length), s, -jnp.inf)
                 w = jnp.exp(s - jnp.max(s, axis=-1, keepdims=True))
                 z = jnp.sum(w, axis=-1, keepdims=True)
-                c = jnp.dot(w.astype(jnp.bfloat16), vb[p, :keys], preferred_element_type=jnp.float32) / z
+                c = jnp.dot(w.astype(jnp.bfloat16), v_out[i * PC + p, 0, :keys], preferred_element_type=jnp.float32) / z
                 ctx_st[slot, p, b * blk:keys] = c.astype(jnp.bfloat16)
 
         for d in range(1, n):
@@ -262,17 +270,8 @@
     half = wout.shape[0] // 2
     wo_copies = [pltpu.make_async_copy(wout.at[pl.ds(k * half, half)], a_nb.at[k, pl.ds(0, half)], wo_sem.at[k]) for k in range(2)]
 
-    def store(i, slot):
-        return pltpu.make_async_copy(out_b.at[slot], out.at[chunk(i)], o_sem.at[slot])
-
     def finish_chunk(i):
-        slot = lax.rem(i, 2)
         await_bytes(ctx_rv.at[pl.ds(0, n - 1), chunk(0)], c_recv.at[i])
-
-        @pl.when(i >= 2)
-        def _():
-            store(i - 2, slot).wait()
-
         width = d_model // 4
         ctx = [jnp.concatenate([ctx_rv[k * (n // 2) + h, chunk(i)].reshape(rows, hd) for h in range(n // 2)], axis=1) for k in range(2)]
         for t in range(4):
@@ -280,8 +279,7 @@
             y = acc[chunk_rows(i), cols]
             for k in range(2):
                 y = y + jnp.dot(ctx[k], a_nb[k, :half, cols], preferred_element_type=jnp.float32)
-            out_b[slot, :, :, cols] = y.astype(jnp.bfloat16).reshape(PC, tok, width)
-        store(i, slot).start()
+            out[chunk(i), :, cols] = y.astype(jnp.bfloat16).reshape(PC, tok, width)
 
     @pl.loop(0, n_chunks + 2)
     def _(i):
@@ -326,7 +324,6 @@
 
     for slot in range(2):
         await_bytes(ctx_st.at[slot, :, pl.ds(0, (n - 1) * tok)], c_send.at[slot])
-        store(n_chunks - 2 + slot, (n_chunks + slot) % 2).wait()
 
     @pl.loop(0, n_chunks)
     def _(i):
@@ -334,25 +331,15 @@
             a_copy(side, i).wait_send()
 
 
-def hand_on_kernel(a, b, c, a_out, b_out, c_out, a_v, b_v, c_v, in_sem, out_sem):
-    parts = in_sem.shape[1]
+def hand_on_kernel(a, b, c, a_out, b_out, c_out, sem):
+    parts = sem.shape[1]
     size = a.shape[0] // parts
-    trio = ((a, a_v, a_out), (b, b_v, b_out), (c, c_v, c_out))
-
-    def copies(t, p):
-        src, mid, dst = trio[t]
-        s = pl.ds(p * size, size)
-        return (pltpu.make_async_copy(src.at[s], mid.at[s], in_sem.at[t, p]),
-                pltpu.make_async_copy(mid.at[s], dst.at[s], out_sem.at[t, p]))
-
-    steps = [(t, p) for p in range(parts) for t in range(3)]
-    for s in steps:
-        copies(*s)[0].start()
-    for s in steps:
-        copies(*s)[0].wait()
-        copies(*s)[1].start()
-    for s in steps:
-        copies(*s)[1].wait()
+    copies = [pltpu.make_async_copy(src.at[pl.ds(p * size, size)], dst.at[pl.ds(p * size, size)], sem.at[t, p])
+              for p in range(parts) for t, (src, dst) in enumerate(((a, a_out), (b, b_out), (c, c_out)))]
+    for copy in copies:
+        copy.start()
+    for copy in copies:
+        copy.wait()
 
 
 def solution(mesh):
@@ -380,24 +367,23 @@
         q, k, v, out = pl.pallas_call(
             functools.partial(layer_kernel, n),
             name='layer',
-            out_shape=(cache, cache, cache, like_out),
+            out_shape=(cache, pltpu.VMEM(cache.shape, bf), pltpu.VMEM(cache.shape, bf), pltpu.VMEM(like_out.shape, bf)),
             in_specs=[SM, ANY, VM, VM, VM, VM, ANY, VM, VM, VM, VM, ANY, VM, ANY, VM, ANY, VM],
-            out_specs=(ANY, ANY, ANY, ANY),
+            out_specs=(ANY, VM, VM, VM),
             scratch_shapes=[
                 pltpu.VMEM((n_rows, d_model), bf),
                 pltpu.VMEM((2, max(n_rows, w_out.shape[0] // 2), d_model), bf),
                 pltpu.VMEM((n_prompts, tok, d_model), bf),
                 pltpu.VMEM((n_rows, d_model), f32),
-                pltpu.VMEM((2 * n_far + 2, d_model, 3 * hd), bf),
+                pltpu.VMEM((W_SLOTS, d_model, 3 * hd), bf),
                 pltpu.VMEM((2, d_model, fb), bf),
                 pltpu.VMEM((2, fb, d_model), bf),
                 pltpu.VMEM((2, 2 * n_far + 6, 3, PC, tok, hd), bf),
-                pltpu.VMEM((PC, seq, hd), bf), pltpu.VMEM((PC, seq, hd), bf), pltpu.VMEM((PC, seq, hd), bf),
+                pltpu.VMEM((PC, seq, hd), bf),
                 pltpu.VMEM((2, PC, seq, hd), bf),
                 pltpu.VMEM((n, n_prompts, tok, hd), bf),
-                pltpu.VMEM((2, PC, tok, d_model), bf),
-                dma((n_chunks,)), dma((2 * n_far + 2,)), dma((2,)), dma((2,)), dma((2, n_chunks)), dma((2, n_chunks)),
-                dma((2,)), dma((2,)), dma((3, n_chunks)), dma((3,)), dma((2,)), dma((n_chunks,)), dma((2,)), dma((2,)),
+                dma((n_chunks,)), dma((W_SLOTS,)), dma((2,)), dma((2,)), dma((2, n_chunks)), dma((2, n_chunks)),
+                dma((2,)), dma((2,)), dma((3, n_chunks)), dma(()), dma((2,)), dma((n_chunks,)), dma((2,)),
             ],
             compiler_params=pltpu.CompilerParams(collective_id=0, has_side_effects=True, vmem_limit_bytes=VMEM_LIMIT),
             cost_estimate=pl.CostEstimate(flops=2 * n_rows * d_model * (4 * d_model + 2 * d_ff), bytes_accessed=200_000_000, transcendentals=0),
@@ -408,12 +394,11 @@
             hand_on_kernel,
             name='hand_on',
             out_shape=(like_out, cache, cache),
-            in_specs=[ANY] * 3,
+            in_specs=[VM] * 3,
             out_specs=(ANY,) * 3,
-            scratch_shapes=[pltpu.VMEM(like_out.shape, bf), pltpu.VMEM(cache.shape, bf), pltpu.VMEM(cache.shape, bf),
-                            dma((3, parts)), dma((3, parts))],
-            compiler_params=pltpu.CompilerParams(vmem_limit_bytes=VMEM_LIMIT),
-        )(out, k, v)
+            scratch_shapes=[dma((3, parts))],
+            compiler_params=pltpu.CompilerParams(vmem_limit_bytes=1 << 20),
+        )(*(pltpu.with_memory_space_constraint(t, pltpu.VMEM) for t in (out, k, v)))
 
     return jax.shard_map(local_layer, mesh=mesh,
                          in_specs=(row_spec, P('dp'), vec_spec, vec_spec, vec_spec, vec_spec, mat_spec, P(None, None, None), mat_spec, vec_spec, mat_spec, vec_spec, mat_spec, vec_spec),

time: 358 us -> 353 us (0.986)
  Pallas kernels: 356 us -> 350 us
    pallas_call x1, Pallas kernels: 9.2 us -> 4.67 us  [local_layer(): pl.pallas_call(hand_on_kernel, name='hand_on', out_shape=(like_out, cache...]
where the time goes in v3:
time: 353 us; the launch traced here: 351 us
  Pallas kernels  350 us (99%)
    pallas_call x1, Pallas kernels, local_layer(): pl.pallas_call(functools.partial(layer_kernel, n), name='layer', out_shap...  346 us

profile of v3, /device:TPU:21, one launch (start us, length us, event | category | flops | bytes accessed | tf_op | source)
XLA Modules:
  0.0 350.8 jit_solution(597292438977798248)
XLA Ops:
  0.6 345.5 %layer.1 = (bf16[32,1,512,128]{3,2,1,0:T(8,128)(2,1)}, bf16[32,1,512,128]{3,2,1,0:T(8,128)(2,1)S(1)}, bf16[32,1,512,128]{3,2,1,0:T(8,128)(2,1)S(1)}, bf16[32,32,2048]{2,1,0:T(8,128)(2,1)S(1)}) custom-call(s32[32]{0:T(128)} %lens.1, bf16[32,32,2048]{2,1,0:T(8,128)(2,1)} %hid.1, f32[1,2048]{1,0:T(1,128)} %bitcast.10, f32[1,2048]{1,0:T(1,128)} %bitcast.11, ...), custom_call_target="tpu_custom_call" | custom-call | flops 103079215104 | bytes 200000000 | tf_op jit(solution)/shard_map/layer/pallas_call | solution.py:367
  346.1 4.7 %hand_on.1 = (bf16[32,32,2048]{2,1,0:T(8,128)(2,1)}, bf16[32,1,512,128]{3,2,1,0:T(8,128)(2,1)}, bf16[32,1,512,128]{3,2,1,0:T(8,128)(2,1)}) custom-call(bf16[32,32,2048]{2,1,0:T(8,128)(2,1)S(1)} %get-tuple-element.6.a, bf16[32,1,512,128]{3,2,1,0:T(8,128)(2,1)S(1)} %get-tuple-element.7.b, bf16[32,1,512,128]{3,2,1,0:T(8,128)(2,1)S(1)} %get-tuple-element.8.c), custom_call_target="tpu_custom_call" | custom-call | tf_op jit(solution)/shard_map/hand_on/pallas_call | solution.py:393

commit v4 on v3

v4 whole, which is shorter than its diff:
```python
import functools

import jax
import jax.numpy as jnp
import numpy as np
from jax import lax
from jax.experimental import pallas as pl
from jax.experimental.pallas import tpu as pltpu
from jax.sharding import PartitionSpec as P

LN_EPS = 1e-5
ROT_BASE = 10000.0
PC = 4
AHEAD = 3
FB = 512
W_SLOTS = 4
HOME = 2
MESH = pl.DeviceIdType.MESH
VMEM_LIMIT = 54_400_000
ANY = pl.BlockSpec(memory_space=pl.ANY)
VM = pl.BlockSpec(memory_space=pltpu.VMEM)
SM = pl.BlockSpec(memory_space=pltpu.SMEM)


def rotary_tables(seq_len, head_dim):
    rot = head_dim // 4
    half = rot // 2
    inv = np.float32(ROT_BASE) ** (np.float32(-2.0) * np.arange(half, dtype=np.float32) / np.float32(rot))
    ang = np.arange(seq_len, dtype=np.float32)[:, None] * inv[None, :].astype(np.float32)
    cos, sin = np.cos(ang), np.sin(ang)
    c = np.ones((seq_len, head_dim), np.float32)
    s = np.zeros((2, seq_len, head_dim), np.float32)
    c[:, :half] = cos
    c[:, half:rot] = cos
    s[0, :, :half] = -sin
    s[1, :, half:rot] = sin
    return np.stack([c, s[0], s[1]])


def entry_barrier(n, me):
    sem = pltpu.get_barrier_semaphore()
    for d in range(1, n):
        pl.semaphore_signal(sem, inc=1, device_id={'sp': lax.rem(me + d, n)}, device_id_type=MESH)
    return lambda: pl.semaphore_wait(sem, n - 1)


def layer_kernel(n, lens, hid, g1, s1, g2, s2, wqkv, bqkv, tabs, wup, bup, wdn, bdn, wout, bout,
                 q_out, k_out, v_out, out, p_rows,
                 a_own, a_nb, m_buf, acc, w_sc, wup_b, wdn_b, st, qb, ctx_st, ctx_rv, p_buf, hq, hk, hv, h_st, tab,
                 x_sem, w_sem, up_sem, dn_sem, a_send, a_recv, st_sem, self_sem, r_sem, in_sem, c_send, c_recv, wo_sem, p_send, p_recv, p_sem, h_send, t_sem):
    me = lax.axis_index('sp')
    chip = lax.div(me, 2)
    n_prompts, tok, d_model = hid.shape
    seq, hd = q_out.shape[2], q_out.shape[3]
    wide = 3 * hd
    n_chunks = n_prompts // PC
    rows = PC * tok
    n_far = n // 2 - 3
    n_w = 2 * n_far + 2
    n_slots = w_sc.shape[0]
    n_remote = 2 * n_far + 3
    n_fb, fb = bup.shape[0], bup.shape[2]
    per_tick = n_fb // n_chunks
    outs = (q_out, k_out, v_out)
    scale = np.float32(hd ** -0.5)
    below = lax.rem(me + n - 2, n)
    above = lax.rem(me + 2, n)

    core = lax.rem(me, 2)
    partner = me + 1 - 2 * core
    beside = lax.rem(partner + n - 2, n)
    n_home = 2 * HOME
    at_home = me < n_home
    home_tok = n_home * tok
    n_own = n // 2
    n_stay = (below < n_home).astype(jnp.int32) + at_home.astype(jnp.int32) + (above < n_home).astype(jnp.int32)

    def by_stay(do):
        for v in range(3):
            pl.when(n_stay == v)(functools.partial(do, v))

    await_barrier = entry_barrier(n, me)

    def chunk_rows(i):
        return pl.ds(pl.multiple_of(i * rows, rows), rows)

    def chunk(i):
        return pl.ds(i * PC, PC)

    def tokens_of(s):
        return pl.ds(pl.multiple_of(s * tok, tok), tok)

    def await_bytes(ref, sem):
        pltpu.make_async_copy(ref, ref, sem).wait()

    def x_copy(i):
        return pltpu.make_async_copy(hid.at[chunk(i)], m_buf.at[chunk(i)], x_sem.at[i])

    def head_at(j):
        return lax.rem(2 * chip - n_far + j + n, n)

    def w_copy(k):
        j = jnp.where(k < 2 * n_far, jnp.where(lax.rem(k, 2) == 0, n_w - 1 - lax.div(k, 2), lax.div(k, 2)),
                      n_far + jnp.where(k == 2 * n_far, 1 - core, core))
        head = jnp.where(k < n_w, head_at(j), n_own * core + k - n_w)
        cols = pl.ds(pl.multiple_of(head * wide, 128), wide)
        slot = lax.rem(k, n_slots)
        return pltpu.make_async_copy(wqkv.at[:, cols], w_sc.at[slot], w_sem.at[slot])

    last_tick = n_chunks - 1 + jnp.where(at_home, 2, 0)

    def next_weights(i, k):
        after = k + n_slots
        end = jnp.where(at_home & (i >= 2), n_w + n_own, n_w)
        start = jnp.where(i + 1 < n_chunks, 0, n_w)

        @pl.when((after < end) | (i < last_tick))
        def _():
            w_copy(jnp.where(after < end, after, start + after - end)).start()

    def up_copy(j, slot):
        return pltpu.make_async_copy(wup.at[:, pl.ds(pl.multiple_of(j * fb, 128), fb)], wup_b.at[slot], up_sem.at[slot])

    def dn_copy(j, slot):
        return pltpu.make_async_copy(wdn.at[pl.ds(pl.multiple_of(j * fb, 128), fb)], wdn_b.at[slot], dn_sem.at[slot])

    sources = (below, me, above, beside, partner)
    tab_copies = [pltpu.make_async_copy(tabs.at[:, tokens_of(src)], tab.at[g], t_sem.at[g]) for g, src in enumerate(sources)]

    @pl.loop(0, n_chunks)
    def _(i):
        x_copy(i).start()

    @pl.loop(0, n_slots)
    def _(k):
        w_copy(k).start()

    for c in tab_copies:
        c.start()

    for j in range(2):
        up_copy(j, j).start()
        dn_copy(j, j).start()

    def a_copy(side, i):
        return pltpu.make_async_remote_copy(
            src_ref=a_own.at[chunk_rows(i)], dst_ref=a_nb.at[side, chunk_rows(i)], send_sem=a_send.at[side, i],
            recv_sem=a_recv.at[side, i], device_id={'sp': above if side == 0 else below}, device_id_type=MESH)

    def norm_chunk(i):
        x_copy(i).wait()

        @pl.loop(0, PC)
        def _(p):
            b = i * PC + p
            r = pl.ds(pl.multiple_of(b * tok, tok), tok)
            x = m_buf[b].astype(jnp.float32)
            cen = x - jnp.mean(x, axis=-1, keepdims=True)
            var = jnp.mean(cen * cen, axis=-1, keepdims=True)
            nor = cen * lax.rsqrt(var + LN_EPS)
            a_own[r] = (nor * g1[...] + s1[...]).astype(jnp.bfloat16)
            m_buf[b] = (nor * g2[...] + s2[...]).astype(jnp.bfloat16)
            acc[r] = x + (bout[...] + bdn[...])

    norm_chunk(0)
    await_barrier()
    for side in range(2):
        a_copy(side, 0).start()

    @pl.loop(1, n_chunks)
    def _(i):
        norm_chunk(i)

        @pl.when(i < AHEAD)
        def _():
            for side in range(2):
                a_copy(side, i).start()

    def finish_block(y, head, g, put, parts=(0, 1, 2)):
        cc, cl, cr = (tab[g, t][None] for t in range(3))
        for m in parts:
            u = y[:, (m - parts[0]) * hd:(m - parts[0] + 1) * hd] + bqkv[m, pl.ds(head, 1)]
            if m < 2:
                far = pltpu.roll(u, hd - hd // 8, 1).reshape(PC, tok, hd)
                near = pltpu.roll(u, hd // 8, 1).reshape(PC, tok, hd)
                u = u.reshape(PC, tok, hd) * cc + far * cl + near * cr
            else:
                u = u.reshape(PC, tok, hd)
            put(m, u.astype(jnp.bfloat16))

    def stage(slot, blk):
        def put(m, u):
            st[slot, blk, m] = u
        return put

    def place(m, i, src):
        return outs[m].at[chunk(i), 0, tokens_of(src)]

    def send_block(i, src, slot, blk, dest):
        def send(m):
            pltpu.make_async_remote_copy(
                src_ref=st.at[slot, blk, m], dst_ref=place(m, i, src), send_sem=st_sem.at[slot, min(m, 1)],
                recv_sem=r_sem.at[m, i], device_id={'sp': dest}, device_id_type=MESH).start()
        pl.when(src >= n_home)(lambda: send(0))
        send(1)
        send(2)

    def free_slot(slot):
        await_bytes(st.at[slot, pl.ds(0, n_remote), pl.ds(0, 2)], st_sem.at[slot, 1])
        await_bytes(st.at[slot, pl.ds(0, 3), pl.ds(0, 2)], self_sem.at[slot, 1])

        def queries(v):
            await_bytes(st.at[slot, pl.ds(0, (n_far if v else 2 * n_far) + 3 - v), 0], st_sem.at[slot, 0])
            await_bytes(st.at[slot, pl.ds(0, 3 - v), 0], self_sem.at[slot, 0])
        by_stay(queries)

    def p_copy(b, i):
        src = a_own.at[chunk_rows(i)] if b == 0 else a_nb.at[0, chunk_rows(i)]
        return pltpu.make_async_remote_copy(
            src_ref=src, dst_ref=p_rows.at[b, chunk_rows(i)], send_sem=p_send.at[b, i], recv_sem=p_recv.at[b, i],
            device_id={'sp': partner}, device_id_type=MESH)

    def project_chunk(i):
        slot = lax.rem(i, 2)
        r = chunk_rows(i)

        for side in range(2):
            a_copy(side, i).wait_recv()

        @pl.when(at_home)
        def _():
            for b in range(2):
                p_copy(b, i).start()

        @pl.loop(0, n_far)
        def _(t):
            ends = ((below, n_w - 1 - t), (above, t))
            for side in range(2):
                w_copy(2 * t + side).wait()
            y = [jnp.dot(a_nb[side, r], w_sc[lax.rem(2 * t + side, n_slots)], preferred_element_type=jnp.float32) for side in range(2)]
            for side, (src, j) in enumerate(ends):
                finish_block(y[side], head_at(j), 2 * side, stage(slot, side * n_far + t))
            for side, (src, j) in enumerate(ends):
                send_block(i, src, slot, side * n_far + t, head_at(j))
            for side in range(2):
                next_weights(i, 2 * t + side)

        @pl.loop(0, 2)
        def _(q):
            dest = 2 * chip + jnp.where(q == 1, core, 1 - core)
            k = 2 * n_far + q
            w_copy(k).wait()
            for g, src in enumerate((below, me, above)):
                rows_in = a_own[r] if g == 1 else a_nb[g // 2, r]
                y = jnp.dot(rows_in, w_sc[lax.rem(k, n_slots)], preferred_element_type=jnp.float32)
                finish_block(y, dest, g, stage(slot, 2 * n_far + 3 * q + g))
            next_weights(i, k)

            @pl.when(q == 0)
            def _():
                for g, src in enumerate((below, me, above)):
                    send_block(i, src, slot, 2 * n_far + g, dest)

            @pl.when(q == 1)
            def _():
                for g, src in enumerate((below, me, above)):
                    def keep(m, g=g, src=src):
                        pltpu.make_async_copy(st.at[slot, n_remote + g, m], place(m, i, src), self_sem.at[slot, min(m, 1)]).start()
                    pl.when(src >= n_home)(functools.partial(keep, 0))
                    keep(1)
                    keep(2)

    def mlp_block(j):
        slot = lax.rem(j, 2)
        up_copy(j, slot).wait()
        dn_copy(j, slot).wait()
        mp = 2 * PC

        @pl.loop(0, n_prompts // mp)
        def _(r):
            rr = pl.ds(pl.multiple_of(r * mp * tok, mp * tok), mp * tok)
            x = m_buf[pl.ds(r * mp, mp)].reshape(mp * tok, d_model)
            pre = jnp.dot(x, wup_b[slot], preferred_element_type=jnp.float32) + bup[j]
            act = (0.5 * pre * (1.0 + lax.erf(pre * np.float32(np.sqrt(0.5))))).astype(jnp.bfloat16)
            acc[rr] += jnp.dot(act, wdn_b[slot], preferred_element_type=jnp.float32)

        @pl.when(j + 2 < n_fb)
        def _():
            up_copy(j + 2, slot).start()
            dn_copy(j + 2, slot).start()

    blk = seq // 2

    def q_load(i):
        return pltpu.make_async_copy(q_out.at[chunk(i), 0, pl.ds(home_tok, seq - home_tok)], qb, in_sem)

    def free_ctx(slot):
        for home in range(2):
            @pl.when(at_home == bool(home))
            def _():
                await_bytes(ctx_st.at[slot, :, pl.ds(0, (n - n_home - 1 + home) * tok)], c_send.at[slot])

    def p_load(b, i):
        return pltpu.make_async_copy(p_rows.at[b, chunk_rows(i)], p_buf.at[b], p_sem.at[b])

    def gather_chunk(i):
        @pl.when(at_home)
        def _():
            for b in range(2):
                p_copy(b, i).wait_recv()
                p_load(b, i).start()

        for m in range(1, 3):
            await_bytes(outs[m].at[chunk(0), 0, pl.ds(0, (n - 3) * tok)], r_sem.at[m, i])
        by_stay(lambda v: await_bytes(q_out.at[chunk(0), 0, pl.ds(0, (n - n_home - 3 + v) * tok)], r_sem.at[0, i]))
        q_load(i).start()

    def attend_chunk(i):
        slot = lax.rem(i, 2)

        @pl.when(i >= 2)
        def _():
            free_ctx(slot)

        q_load(i).wait()

        @pl.loop(0, PC)
        def _(p):
            length = lens[i * PC + p]
            for b in range(2):
                keys = (b + 1) * blk
                first = max(b * blk, home_tok)
                s = lax.dot_general(qb[p, first - home_tok:keys - home_tok], k_out[i * PC + p, 0, :keys], (((1,), (1,)), ((), ())),
                                    preferred_element_type=jnp.float32) * scale
                key = lax.broadcasted_iota(jnp.int32, (keys - first, keys), 1)
                row = lax.broadcasted_iota(jnp.int32, (keys - first, keys), 0) + first
                s = jnp.where((key <= row) & (key < length), s, -jnp.inf)
                w = jnp.exp(s - jnp.max(s, axis=-1, keepdims=True))
                z = jnp.sum(w, axis=-1, keepdims=True)
                c = jnp.dot(w.astype(jnp.bfloat16), v_out[i * PC + p, 0, :keys], preferred_element_type=jnp.float32) / z
                ctx_st[slot, p, first - home_tok:keys - home_tok] = c.astype(jnp.bfloat16)

        for d in range(1, n):
            dest = lax.rem(me + d, n)

            @pl.when(dest >= n_home)
            def _():
                pltpu.make_async_remote_copy(
                    src_ref=ctx_st.at[slot, :, tokens_of(dest - n_home)], dst_ref=ctx_rv.at[me, chunk(i)],
                    send_sem=c_send.at[slot], recv_sem=c_recv.at[i], device_id={'sp': dest}, device_id_type=MESH).start()

        @pl.when(me >= n_home)
        def _():
            ctx_rv[me, chunk(i)] = ctx_st[slot, :, tokens_of(me - n_home)]

    def h_copy(i, slot):
        return pltpu.make_async_remote_copy(
            src_ref=h_st.at[slot], dst_ref=ctx_rv.at[pl.ds(n_own * core, n_own), chunk(i)], send_sem=h_send.at[slot],
            recv_sem=c_recv.at[i], device_id={'sp': partner}, device_id_type=MESH)

    def home_chunk(i):
        slot = lax.rem(i, 2)
        r = chunk_rows(i)
        @pl.when(i >= 2)
        def _():
            h_copy(i - 2, slot).wait_send()

        for b in range(2):
            p_load(b, i).wait()

        kinds = (below, beside, me, partner)

        def positions(shards, shape, dim):
            t = lax.broadcasted_iota(jnp.int32, shape, dim)
            pos = t + shards[0] * tok
            for b in range(1, len(shards)):
                pos = jnp.where(t >= b * tok, t + (shards[b] - b) * tok, pos)
            return pos

        key = positions(kinds, (2 * tok, 4 * tok), 1)
        row = positions(kinds[2:], (2 * tok, 4 * tok), 0)

        def project_head(h):
            w = w_sc.at[lax.rem(n_w + h, n_slots)]
            par = lax.rem(h, 2)
            own = jnp.dot(jnp.concatenate([a_own[r], p_buf[0]], axis=0), w[...], preferred_element_type=jnp.float32)
            old = jnp.dot(jnp.concatenate([a_nb[0, r], p_buf[1]], axis=0), w[:, hd:], preferred_element_type=jnp.float32)
            for b in range(4):
                def put(m, u, b=b):
                    (hq, hk, hv)[m][par, b - 2 if m == 0 else b] = u
                y = (old if b < 2 else own)[b % 2 * rows:(b % 2 + 1) * rows]
                finish_block(y, n_own * core + h, (0, 3, 1, 4)[b], put, (0, 1, 2) if b >= 2 else (1, 2))

        def attend_head(h):
            par = lax.rem(h, 2)
            head = n_own * core + h
            s = [lax.dot_general(hq[par, :, p].reshape(2 * tok, hd), hk[par, :, p].reshape(4 * tok, hd), (((1,), (1,)), ((), ())),
                                 preferred_element_type=jnp.float32) * scale for p in range(PC)]
            s = [jnp.where((key <= row) & (key < lens[i * PC + p]), s[p], -jnp.inf) for p in range(PC)]
            w = [jnp.exp(t - jnp.max(t, axis=-1, keepdims=True)) for t in s]
            z = [jnp.sum(t, axis=-1, keepdims=True) for t in w]
            for p in range(PC):
                c = jnp.dot(w[p].astype(jnp.bfloat16), hv[par, :, p].reshape(4 * tok, hd), preferred_element_type=jnp.float32) / z[p]
                c = c.astype(jnp.bfloat16)
                ctx_rv[head, i * PC + p] = c[:tok]
                h_st[slot, h, p] = c[tok:]

        w_copy(n_w).wait()
        project_head(0)
        next_weights(i + 2, n_w)

        @pl.loop(1, n_own)
        def _(h):
            w_copy(n_w + h).wait()
            attend_head(h - 1)
            project_head(h)
            next_weights(i + 2, n_w + h)
        attend_head(n_own - 1)
        h_copy(i, slot).start()

    for c in tab_copies:
        c.wait()

    n_blk = d_model // fb
    wo_copies = []
    for t in range(n_blk):
        cols = pl.ds(t * fb, fb)
        if t < 2:
            wo_copies.append(pltpu.make_async_copy(wout.at[:, cols], wup_b.at[t], up_sem.at[t]))
        else:
            for k in range(n_blk):
                wo_copies.append(pltpu.make_async_copy(wout.at[pl.ds(k * fb, fb), cols], wdn_b.at[t - 2, :, pl.ds(k * fb, fb)], wo_sem.at[t - 2, k]))

    def finish_chunk(i):
        for home in range(2):
            @pl.when(at_home == bool(home))
            def _():
                await_bytes(ctx_rv.at[pl.ds(0, n_own if home else n - 1), chunk(0)], c_recv.at[i])
        ctx = jnp.concatenate([ctx_rv[h, chunk(i)].reshape(rows, hd) for h in range(n)], axis=1)
        for t in range(n_blk):
            cols = slice(t * fb, (t + 1) * fb)
            y = acc[chunk_rows(i), cols]
            if t < 2:
                y = y + jnp.dot(ctx, wup_b[t], preferred_element_type=jnp.float32)
            else:
                w = jnp.concatenate([wdn_b[t - 2, :, k * fb:(k + 1) * fb] for k in range(n_blk)], axis=0)
                y = y + jnp.dot(ctx, w, preferred_element_type=jnp.float32)
            out[chunk(i), :, cols] = y.astype(jnp.bfloat16).reshape(PC, tok, fb)

    @pl.loop(0, n_chunks + 2)
    def _(i):
        @pl.when(i + AHEAD < n_chunks)
        def _():
            for side in range(2):
                a_copy(side, i + AHEAD).start()

        @pl.when(i >= 2)
        def _():
            free_slot(lax.rem(i, 2))

        @pl.when(i < n_chunks)
        def _():
            project_chunk(i)

        @pl.when(i >= 2)
        def _():
            gather_chunk(i - 2)

        @pl.when(i < n_chunks)
        def _():
            @pl.loop(0, per_tick)
            def _(j):
                mlp_block(i * per_tick + j)

            @pl.when(i == n_chunks - 1)
            def _():
                for c in wo_copies:
                    c.start()

        @pl.when(i >= 2)
        def _():
            attend_chunk(i - 2)

            @pl.when(at_home)
            def _():
                home_chunk(i - 2)

        @pl.when(i == n_chunks)
        def _():
            for c in wo_copies:
                c.wait()

            @pl.loop(0, n_chunks - 3)
            def _(j):
                finish_chunk(j)

    @pl.loop(n_chunks - 3, n_chunks)
    def _(j):
        finish_chunk(j)

    for slot in range(2):
        free_ctx(slot)

        @pl.when(at_home)
        def _():
            h_copy(n_chunks - 2 + slot, (n_chunks + slot) % 2).wait_send()
            for b in range(2):
                @pl.loop(slot, n_chunks, step=2)
                def _(j):
                    p_copy(b, j).wait_send()

    @pl.loop(0, n_chunks)
    def _(i):
        for side in range(2):
            a_copy(side, i).wait_send()


def hand_on_kernel(a, b, c, a_out, b_out, c_out, sem):
    parts = sem.shape[1]
    size = a.shape[0] // parts
    copies = [pltpu.make_async_copy(src.at[pl.ds(p * size, size)], dst.at[pl.ds(p * size, size)], sem.at[t, p])
              for p in range(parts) for t, (src, dst) in enumerate(((a, a_out), (b, b_out), (c, c_out)))]
    for copy in copies:
        copy.start()
    for copy in copies:
        copy.wait()


def solution(mesh):
    n = mesh.shape['sp']
    row_spec = P('dp', 'sp', None)
    cache_spec = P('dp', 'sp', None, None)
    vec_spec = P(None)
    mat_spec = P(None, None)

    def local_layer(hidden, seq_lens, ln1_gain, ln1_bias, ln2_gain, ln2_bias, w_qkv, b_qkv, w_out, b_out, w_up, b_up, w_down, b_down):
        n_prompts, tok, d_model = hidden.shape
        hd = b_qkv.shape[2]
        d_ff = w_up.shape[1]
        seq = tok * n
        n_rows = n_prompts * tok
        n_chunks = n_prompts // PC
        rows = PC * tok
        fb = min(FB, d_ff // n_chunks)
        n_far = n // 2 - 3
        bf, f32 = jnp.bfloat16, jnp.float32
        row = lambda v: v.reshape(1, d_model)
        tabs = jnp.asarray(rotary_tables(seq, hd))
        cache = jax.ShapeDtypeStruct((n_prompts, 1, seq, hd), bf)
        like_out = jax.ShapeDtypeStruct((n_prompts, tok, d_model), bf)
        dma = pltpu.SemaphoreType.DMA
        q, k, v, out, _ = pl.pallas_call(
            functools.partial(layer_kernel, n),
            name='layer',
            out_shape=(cache, pltpu.VMEM(cache.shape, bf), pltpu.VMEM(cache.shape, bf), pltpu.VMEM(like_out.shape, bf),
                       jax.ShapeDtypeStruct((2, n_rows, d_model), bf)),
            in_specs=[SM, ANY, VM, VM, VM, VM, ANY, VM, ANY, ANY, VM, ANY, VM, ANY, VM],
            out_specs=(ANY, VM, VM, VM, ANY),
            scratch_shapes=[
                pltpu.VMEM((n_rows, d_model), bf),
                pltpu.VMEM((2, n_rows, d_model), bf),
                pltpu.VMEM((n_prompts, tok, d_model), bf),
                pltpu.VMEM((n_rows, d_model), f32),
                pltpu.VMEM((W_SLOTS, d_model, 3 * hd), bf),
                pltpu.VMEM((2, d_model, fb), bf),
                pltpu.VMEM((2, fb, d_model), bf),
                pltpu.VMEM((2, 2 * n_far + 6, 3, PC, tok, hd), bf),
                pltpu.VMEM((PC, seq - 2 * HOME * tok, hd), bf),
                pltpu.VMEM((2, PC, seq - 2 * HOME * tok, hd), bf),
                pltpu.VMEM((n, n_prompts, tok, hd), bf),
                pltpu.VMEM((2, rows, d_model), bf),
                pltpu.VMEM((2, 2, PC, tok, hd), bf), pltpu.VMEM((2, 4, PC, tok, hd), bf), pltpu.VMEM((2, 4, PC, tok, hd), bf),
                pltpu.VMEM((2, n // 2, PC, tok, hd), bf),
                pltpu.VMEM((5, 3, tok, hd), f32),
                dma((n_chunks,)), dma((W_SLOTS,)), dma((2,)), dma((2,)), dma((2, n_chunks)), dma((2, n_chunks)),
                dma((2, 2)), dma((2, 2)), dma((3, n_chunks)), dma(()), dma((2,)), dma((n_chunks,)), dma((2, d_model // fb)),
                dma((2, n_chunks)), dma((2, n_chunks)), dma((2,)), dma((2,)), dma((5,)),
            ],
            compiler_params=pltpu.CompilerParams(collective_id=0, has_side_effects=True, vmem_limit_bytes=VMEM_LIMIT),
            cost_estimate=pl.CostEstimate(flops=2 * n_rows * d_model * (4 * d_model + 2 * d_ff), bytes_accessed=200_000_000, transcendentals=0),
        )(seq_lens, hidden, row(ln1_gain), row(ln1_bias), row(ln2_gain), row(ln2_bias), w_qkv, jnp.transpose(b_qkv, (1, 0, 2)), tabs,
          w_up, b_up.reshape(d_ff // fb, 1, fb), w_down, row(b_down), w_out, row(b_out))
        parts = 4
        return pl.pallas_call(
            hand_on_kernel,
            name='hand_on',
            out_shape=(like_out, cache, cache),
            in_specs=[VM] * 3,
            out_specs=(ANY,) * 3,
            scratch_shapes=[dma((3, parts))],
            compiler_params=pltpu.CompilerParams(vmem_limit_bytes=1 << 20),
        )(*(pltpu.with_memory_space_constraint(t, pltpu.VMEM) for t in (out, k, v)))

    return jax.shard_map(local_layer, mesh=mesh,
                         in_specs=(row_spec, P('dp'), vec_spec, vec_spec, vec_spec, vec_spec, mat_spec, P(None, None, None), mat_spec, vec_spec, mat_spec, vec_spec, mat_spec, vec_spec),
                         out_specs=(row_spec, cache_spec, cache_spec), check_vma=False)
```

time: 353 us -> 336 us (0.952)
  Pallas kernels: 350 us -> 336 us
    pallas_call x1, Pallas kernels: 346 us -> 331 us  [local_layer(): pl.pallas_call(functools.partial(layer_kernel, n), name='layer', out_shap...]
where the time goes in v4:
time: 336 us
  Pallas kernels  336 us (100%)
    pallas_call x1, Pallas kernels, local_layer(): pl.pallas_call(functools.partial(layer_kernel, n), name='layer', out_shap...  331 us

profile of v4, /device:TPU:21, one launch (start us, length us, event | category | flops | bytes accessed | tf_op | source)
XLA Modules:
  0.0 336.2 jit_solution(15311264744314555010)
XLA Ops:
  0.6 330.9 %layer.1 = (bf16[32,1,512,128]{3,2,1,0:T(8,128)(2,1)}, bf16[32,1,512,128]{3,2,1,0:T(8,128)(2,1)S(1)}, bf16[32,1,512,128]{3,2,1,0:T(8,128)(2,1)S(1)}, bf16[32,32,...) custom-call(s32[32]{0:T(128)} %lens.1, bf16[32,32,2048]{2,1,0:T(8,128)(2,1)} %hid.1, f32[1,2048]{1,0:T(1,128)} %bitcast.10, ...), custom_call_target="tpu_custom_call" | custom-call | flops 103079215104 | bytes 200000000 | tf_op jit(solution)/shard_map/layer/pallas_call | solution.py:552
  331.5 4.7 %hand_on.1 = (bf16[32,32,2048]{2,1,0:T(8,128)(2,1)}, bf16[32,1,512,128]{3,2,1,0:T(8,128)(2,1)}, bf16[32,1,512,128]{3,2,1,0:T(8,128)(2,1)}) custom-call(bf16[32,32,2048]{2,1,0:T(8,128)(2,1)S(1)} %get-tuple-element.6.a, bf16[32,1,512,128]{3,2,1,0:T(8,128)(2,1)S(1)} %get-tuple-element.7.b, bf16[32,1,512,128]{3,2,1,0:T(8,128)(2,1)S(1)} %get-tuple-element.8.c), custom_call_target="tpu_custom_call" | custom-call | tf_op jit(solution)/shard_map/hand_on/pallas_call | solution.py:584
